TPU v7x, 32 devices: a whole 2x2x4 slice. The times are simulated.
32 devices in a mesh: row: 4 (over y, x), col: 4 (over z), head: 2 (over core).
Axes of the slice: x: 2, y: 2, z: 4, core: 2. Of those that a mesh axis runs over, the one named last changes fastest.
Arguments:
- queries: bfloat16 [256, 64, 256], P('row', 'col'), may hold values from -1000 to 1000
- level_zero: bfloat16 [256, 64, 256], P('row', 'col', 'head'), may hold values from -6 to 6
- level_one: bfloat16 [128, 32, 256], P('row', 'col', 'head'), may hold values from -6 to 6
- level_two: bfloat16 [64, 16, 256], P('row', 'col', 'head'), may hold values from -6 to 6
- level_three: bfloat16 [32, 8, 256], P('row', 'col', 'head'), may hold values from -6 to 6
- tile_lists: int32 [16, 4, 4, 8], P('row', 'col'), may hold values from 0 to 63, as said below
- samples: int32 [256, 64, 128], P('row', 'col', 'head'), may hold values from 0 to 133168895, as said below
- logit_weight: bfloat16 [256, 128], P(None, 'head'), may hold values from -1 to 1
- logit_bias: float32 [128], P('head'), may hold values from -3 to 3
- output_weight: bfloat16 [256, 256], replicated, may hold values from -0.375 to 0.375
- output_bias: float32 [256], replicated, may hold values from -3 to 3
- norm_gain: float32 [256], P('head'), may hold values from 0.5 to 1.5
- norm_shift: float32 [256], P('head'), may hold values from -3 to 3
Outputs:
- updated_queries: bfloat16 [256, 64, 256], P('row', 'col', 'head')
Inputs may be any that keep to these rules, and one draw needn't show every extreme that they name: `tile_lists`: entries are tile numbers r * 4 + c. Over all lists of the query blocks that one device holds, at one level, at most 2 entries name tiles that one device holds; at each level some device is named exactly 2 times by the lists of every device. A tile may be listed more than once. `samples`: slot is below 8; at level l, pos_row and pos_col are below (16 / 2^l - 1) * 256.
All inputs are finite; a program needn't handle non-finite values.
Results may differ from a plain program's by a relative error of at most 0.004.
Values may be sent and summed in bfloat16 or wider, within the bound.
A program may use at most 128 MiB of HBM per device.

v0:
```python
import jax
import jax.numpy as jnp
from jax import lax
from jax.sharding import PartitionSpec as P

LEVELS = 4
POINTS = 4


def as_sent(array):

    def short(part):
        return part.astype(jnp.bfloat16) if part.dtype == jnp.float32 else part

    return jax.tree.map(short, array)


def to_blocks(source, tile_rows, tile_cols, tile_side):
    channels = source.shape[2]
    shaped = source.reshape(tile_rows, tile_side, tile_cols, tile_side, channels)
    return shaped.transpose(0, 2, 1, 3, 4).reshape(
        tile_rows * tile_cols, tile_side * tile_side, channels
    )


def pixel_weights(attend, packed, tile_side, width_total):
    slot_index = packed // 16777216
    pos_row = packed // 4096 % 4096
    pos_col = packed % 4096
    frac_row = (pos_row % 256).astype(jnp.float32) / 256.0
    frac_col = (pos_col % 256).astype(jnp.float32) / 256.0
    base_index = slot_index * tile_side * tile_side + pos_row // 256 * tile_side + pos_col // 256
    column = jnp.arange(width_total, dtype=jnp.int32)
    combined = jnp.zeros((attend.shape[1], attend.shape[0], width_total), jnp.float32)
    corners = (
        (0, 1.0 - frac_row, 1.0 - frac_col),
        (1, 1.0 - frac_row, frac_col),
        (tile_side, frac_row, 1.0 - frac_col),
        (tile_side + 1, frac_row, frac_col),
    )
    for point_num in range(attend.shape[2]):
        for offset, weight_row, weight_col in corners:
            corner_weight = (
                attend[:, :, point_num] * weight_row[:, :, point_num] * weight_col[:, :, point_num]
            ).T
            target = (base_index[:, :, point_num] + offset).T
            combined = combined + jnp.where(
                column[None, None, :] == target[:, :, None], corner_weight[:, :, None], 0.0
            )
    return combined.astype(jnp.bfloat16)


def on_device(
    queries,
    level_zero,
    level_one,
    level_two,
    level_three,
    tile_lists,
    samples,
    logit_weight,
    logit_bias,
    output_weight,
    output_bias,
    norm_gain,
    norm_shift,
):
    level_blocks = (level_zero, level_one, level_two, level_three)
    row_count = lax.axis_size("row")
    col_count = lax.axis_size("col")
    peer_count = row_count * col_count
    tile_rows, tile_cols, level_count, per_block = tile_lists.shape
    local_tiles = tile_rows * tile_cols
    requests = local_tiles * per_block
    capacity = max(2, (requests + peer_count - 1) // peer_count)
    grid_cols = tile_cols * col_count
    channels = level_zero.shape[2]
    width_all = queries.shape[2]
    head_count = samples.shape[2] // (LEVELS * POINTS)
    head_dim = channels // head_count
    tile_side = level_zero.shape[0] // tile_rows
    pixels = tile_side * tile_side
    tile_sides = [level_blocks[level_num].shape[0] // tile_rows for level_num in range(level_count)]
    tiles_local = []
    send_ids = []
    positions = []
    request_order = jnp.arange(requests, dtype=jnp.int32)
    for level_num in range(level_count):
        side_here = tile_sides[level_num]
        shaped = level_blocks[level_num].reshape(
            tile_rows, side_here, tile_cols, side_here, channels
        )
        tiles_local.append(
            shaped.transpose(0, 2, 1, 3, 4).reshape(local_tiles, side_here, side_here, channels)
        )
        wanted = tile_lists[:, :, level_num, :].reshape(requests)
        grid_row = wanted // grid_cols
        grid_col = wanted % grid_cols
        owner_dev = grid_row // tile_rows * col_count + grid_col // tile_cols
        local_index = grid_row % tile_rows * tile_cols + grid_col % tile_cols
        same_owner = (owner_dev[:, None] == owner_dev[None, :]) & (
            request_order[None, :] < request_order[:, None]
        )
        pair_rank = jnp.sum(same_owner.astype(jnp.int32), axis=1)
        slot_place = owner_dev * capacity + pair_rank
        slot_table = (
            jnp.full((peer_count * capacity,), -1, jnp.int32).at[slot_place].set(local_index)
        )
        send_ids.append(slot_table.reshape(peer_count, capacity))
        positions.append(slot_place)
    received = lax.all_to_all(
        tuple(send_ids), ("row", "col"), split_axis=0, concat_axis=0, tiled=True
    )
    replies = []
    for serve_level_num in range(level_count):
        asked_ids = received[serve_level_num]
        is_valid = asked_ids >= 0
        picked = jnp.take(tiles_local[serve_level_num], jnp.maximum(asked_ids, 0), axis=0)
        replies.append(jnp.where(is_valid[:, :, None, None, None], picked, jnp.zeros_like(picked)))
    fetched = lax.all_to_all(
        as_sent(tuple(replies)), ("row", "col"), split_axis=0, concat_axis=0, tiled=True
    )
    gathered = []
    for level_num in range(level_count):
        side_here = tile_sides[level_num]
        flat_tiles = fetched[level_num].reshape(
            (peer_count * capacity, side_here, side_here, channels)
        )
        chosen = jnp.take(flat_tiles, positions[level_num], axis=0)
        gathered.append(chosen.reshape(local_tiles, per_block * side_here * side_here, channels))
    queries_blocked = to_blocks(queries, tile_rows, tile_cols, tile_side).reshape(
        local_tiles * pixels, width_all
    )
    logits = jnp.dot(queries_blocked, logit_weight, preferred_element_type=jnp.float32) + logit_bias
    attend = jax.nn.softmax(
        logits.reshape(local_tiles * pixels, head_count, LEVELS * POINTS), axis=-1
    )
    attend = attend.reshape(local_tiles, pixels, head_count, LEVELS, POINTS)
    packed = to_blocks(samples, tile_rows, tile_cols, tile_side).reshape(
        local_tiles, pixels, head_count, LEVELS, POINTS
    )

    def block_output(operands):
        attend_blk = operands[0]
        packed_blk = operands[1]
        running = jnp.zeros((pixels, head_count, head_dim), jnp.float32)
        for level_num in range(level_count):
            tile_values = operands[2 + level_num]
            width_total = tile_values.shape[0]
            weights_px = pixel_weights(
                attend_blk[:, :, level_num, :],
                packed_blk[:, :, level_num, :],
                tile_sides[level_num],
                width_total,
            )
            running = running + jnp.einsum(
                "hqn,nhd->qhd",
                weights_px,
                tile_values.reshape(width_total, head_count, head_dim),
                preferred_element_type=jnp.float32,
            )
        return running.reshape(pixels, channels).astype(jnp.bfloat16)

    attn_out = lax.map(
        block_output, (attend, packed, gathered[0], gathered[1], gathered[2], gathered[3])
    )
    attn_out = attn_out.reshape(local_tiles * pixels, channels)
    head_index = lax.axis_index("head")
    full_attn = lax.all_gather(attn_out, "head", axis=1, tiled=True)
    pre_norm = (
        queries_blocked.astype(jnp.float32)
        + jnp.dot(full_attn, output_weight, preferred_element_type=jnp.float32)
        + output_bias
    )
    row_mean = jnp.mean(pre_norm, axis=1, keepdims=True)
    centered = pre_norm - row_mean
    variance = jnp.mean(centered * centered, axis=1, keepdims=True)
    own_part = lax.dynamic_slice_in_dim(centered, head_index * channels, channels, 1)
    normalized = own_part * lax.rsqrt(variance + 1e-05)
    updated = (normalized * norm_gain + norm_shift).astype(jnp.bfloat16)
    updated = updated.reshape(tile_rows, tile_cols, tile_side, tile_side, channels).transpose(
        0, 2, 1, 3, 4
    )
    return updated.reshape(tile_rows * tile_side, tile_cols * tile_side, channels)


def solution(mesh):
    in_specs = (
        P("row", "col", None),
        P("row", "col", "head"),
        P("row", "col", "head"),
        P("row", "col", "head"),
        P("row", "col", "head"),
        P("row", "col", None, None),
        P("row", "col", "head"),
        P(None, "head"),
        P("head"),
        P(),
        P(),
        P("head"),
        P("head"),
    )
    out_specs = P("row", "col", "head")
    return jax.shard_map(
        on_device, mesh=mesh, in_specs=in_specs, out_specs=out_specs, check_vma=False
    )
```

profile of v0, /device:TPU:0, one launch (start us, length us, event | category | flops | bytes accessed | tf_op | source)
XLA Modules:
  0.0 335.1 jit_solution(9578026117994345754)
XLA Ops:
  3.0 8.3 %all-to-all-start.2 = ((s32[16,1,2]{2,1,0:T(1,128)}), s32[16,1,2]{2,1,0:T(1,128)S(1)}, u32[]{:S(2)}, u32[]{:S(2)}) async-start(s32[16,1,2]{2,1,0:T(1,128)} %bitcast.239), calls=%async_computation.2 | async-start | bytes 16384 | tf_op jit(solution)/shard_map/all_to_all | solution.py:111
  18.5 5.6 %all-to-all-start.4 = ((s32[16,1,2]{2,1,0:T(1,128)}), s32[16,1,2]{2,1,0:T(1,128)S(1)}, u32[]{:S(2)}, u32[]{:S(2)}) async-start(s32[16,1,2]{2,1,0:T(1,128)} %bitcast.248), calls=%async_computation.4 | async-start | bytes 16384 | tf_op jit(solution)/shard_map/all_to_all | solution.py:111
  24.3 7.2 %all-to-all-done.4 = s32[16,1,2]{2,1,0:T(1,128)S(1)} async-done(((s32[16,1,2]{2,1,0:T(1,128)}), s32[16,1,2]{2,1,0:T(1,128)S(1)}, u32[]{:S(2)}, u32[]{:S(2)}) %all-to-all-start.4) | async-done | bytes 160 | tf_op jit(solution)/shard_map/all_to_all | solution.py:111
  35.0 7.2 %all-to-all-done.6 = s32[16,1,2]{2,1,0:T(1,128)S(1)} async-done(((s32[16,1,2]{2,1,0:T(1,128)}), s32[16,1,2]{2,1,0:T(1,128)S(1)}, u32[]{:S(2)}, u32[]{:S(2)}) %all-to-all-start.6) | async-done | bytes 160 | tf_op jit(solution)/shard_map/all_to_all | solution.py:111
  52.9 5.1 %all-to-all-start.7 = ((bf16[16,2,2,2,128]{4,3,2,1,0:T(2,128)(2,1)}), bf16[16,2,2,2,128]{4,3,2,1,0:T(2,128)(2,1)S(1)}, u32[]{:S(2)}, u32[]{:S(2)}) async-start(bf16[16,2,2,2,128]{4,3,2,1,0:T(2,128)(2,1)} %broadcast_select_fusion.4), calls=%async_computation.7 | async-start | bytes 65536 | tf_op jit(solution)/shard_map/all_to_all | solution.py:120
  59.5 5.8 %all-to-all-done.7 = bf16[16,2,2,2,128]{4,3,2,1,0:T(2,128)(2,1)S(1)} async-done(((bf16[16,2,2,2,128]{4,3,2,1,0:T(2,128)(2,1)}), bf16[16,2,2,2,128]{4,3,2,1,0:T(2,128)(2,1)S(1)}, u32[]{:S(2)}, u32[]{:S(2)}) %all-to-all-start.7) | async-done | bytes 32800 | tf_op jit(solution)/shard_map/all_to_all | solution.py:120
  69.9 6.6 %all-to-all-done.5 = bf16[16,2,4,4,128]{4,3,2,1,0:T(4,128)(2,1)S(1)} async-done(((bf16[16,2,4,4,128]{4,3,2,1,0:T(4,128)(2,1)}), bf16[16,2,4,4,128]{4,3,2,1,0:T(4,128)(2,1)S(1)}, u32[]{:S(2)}, u32[]{:S(2)}) %all-to-all-start.5) | async-done | bytes 131104 | tf_op jit(solution)/shard_map/all_to_all | solution.py:120
  83.2 8.9 %all-to-all-done.3 = bf16[16,2,8,8,128]{4,3,2,1,0:T(8,128)(2,1)S(1)} async-done(((bf16[16,2,8,8,128]{4,3,2,1,0:T(8,128)(2,1)}), bf16[16,2,8,8,128]{4,3,2,1,0:T(8,128)(2,1)S(1)}, u32[]{:S(2)}, u32[]{:S(2)}) %all-to-all-start.3) | async-done | bytes 524320 | tf_op jit(solution)/shard_map/all_to_all | solution.py:120
  92.0 4.6 %all-to-all-start.1 = ((bf16[16,2,16,16,128]{4,3,2,1,0:T(8,128)(2,1)}), bf16[16,2,16,16,128]{4,3,2,1,0:T(8,128)(2,1)}, u32[]{:S(2)}, u32[]{:S(2)}) async-start(bf16[16,2,16,16,128]{4,3,2,1,0:T(8,128)(2,1)} %select_select_fusion), calls=%async_computation.1 | async-start | bytes 4194304 | tf_op jit(solution)/shard_map/all_to_all | solution.py:120
  112.3 27.3 %all-to-all-done.1 = bf16[16,2,16,16,128]{4,3,2,1,0:T(8,128)(2,1)} async-done(((bf16[16,2,16,16,128]{4,3,2,1,0:T(8,128)(2,1)}), bf16[16,2,16,16,128]{4,3,2,1,0:T(8,128)(2,1)}, u32[]{:S(2)}, u32[]{:S(2)}) %all-to-all-start.1) | async-done | bytes 2097184 | tf_op jit(solution)/shard_map/all_to_all | solution.py:120
  143.3 4.4 %broadcast_select_fusion = bf16[4,2048,128]{2,1,0:T(8,128)(2,1)S(1)} fusion(bf16[4,2048,128]{2,1,0:T(8,128)(2,1)} %bitcast.874, pred[4,2048]{1,0:T(4,128)(4,1)S(1)} %broadcast_in_dim.1051), kind=kLoop, calls=%fused_computation.549 | loop fusion | flops 1048576 | bytes 4202496 | tf_op jit(solution)/shard_map/jit(_take)/select_n | solution.py:129
  147.7 182.1 %while.13 = (s32[]{:T(128)}, bf16[4,256,128]{2,1,0:T(8,128)(2,1)}, bf16[4,2048,128]{2,1,0:T(8,128)(2,1)S(1)}, s32[4,256,4,4,4]{1,0,4,3,2:T(4,128)}, f32[4,256,4,...) while((s32[]{:T(128)}, bf16[4,256,128]{2,1,0:T(8,128)(2,1)}, ...), condition=%wide.region_11.12_spmd, body=%wide.region_10.11_spmd.sunk | while | flops 314474496 | bytes 19226808 | solution.py:164
  154.5 6.5 %fusion.258 = f32[4,32,256]{2,1,0:T(8,128)} fusion(bf16[128,4,32]{0,2,1:T(8,128)(2,1)S(1)} %bitcast.884, f32[4,256]{1,0:T(4,128)S(1)} %get-tuple-element.695, s32[4,256]{1,0:T(4,128)S(1)} %get-tuple-element.696, f32[4,256]{1,0:T(4,128)S(1)} %get-tuple-element.698, s32[4,256]{1,0:T(4,128)S(1)} %get-tuple-element.699, ...), kind=kOutput, calls=%fused_computation.100.clone.1 | convolution fusion | flops 14680064 | bytes 294912 | tf_op jit(solution)/shard_map/while/body/eval_jaxpr/hqn,nhd->qhd/dot_general | solution.py:156
  165.6 18.8 %add_convert_fusion.21 = bf16[4,256,2048]{2,1,0:T(8,128)(2,1)S(1)} fusion(f32[4,256]{1,0:T(4,128)S(1)} %get-tuple-element.732, s32[4,256]{1,0:T(4,128)S(1)} %get-tuple-element.734, f32[4,256]{1,0:T(4,128)S(1)} %get-tuple-element.736, s32[4,256]{1,0:T(4,128)S(1)} %get-tuple-element.737, f32[4,256]{1,0:T(4,128)S(1)} %get-tuple-element.739, ...), kind=kLoop, calls=%fused_computation.12.clone.clone.1.clone.1 | loop fusion | flops 100663296 | bytes 4325376 | tf_op jit(solution)/shard_map/while/body/eval_jaxpr/hqn,nhd->qhd/dot_general | solution.py:156
  186.9 5.1 %add_convert_fusion.22 = bf16[4,256,512]{2,1,0:T(8,128)(2,1)S(1)} fusion(f32[4,256]{1,0:T(4,128)S(1)} %get-tuple-element.771, s32[4,256]{1,0:T(4,128)S(1)} %get-tuple-element.772, f32[4,256]{1,0:T(4,128)S(1)} %get-tuple-element.774, s32[4,256]{1,0:T(4,128)S(1)} %get-tuple-element.775, f32[4,256]{1,0:T(4,128)S(1)} %get-tuple-element.777, ...), kind=kLoop, calls=%fused_computation.30.clone.clone.1.clone.1 | loop fusion | flops 25165824 | bytes 1179648 | tf_op jit(solution)/shard_map/while/body/eval_jaxpr/hqn,nhd->qhd/dot_general | solution.py:156
  200.1 6.5 %fusion.258 = f32[4,32,256]{2,1,0:T(8,128)} fusion(bf16[128,4,32]{0,2,1:T(8,128)(2,1)S(1)} %bitcast.884, f32[4,256]{1,0:T(4,128)S(1)} %get-tuple-element.695, s32[4,256]{1,0:T(4,128)S(1)} %get-tuple-element.696, f32[4,256]{1,0:T(4,128)S(1)} %get-tuple-element.698, s32[4,256]{1,0:T(4,128)S(1)} %get-tuple-element.699, ...), kind=kOutput, calls=%fused_computation.100.clone.1 | convolution fusion | flops 14680064 | bytes 294912 | tf_op jit(solution)/shard_map/while/body/eval_jaxpr/hqn,nhd->qhd/dot_general | solution.py:156
  211.1 18.8 %add_convert_fusion.21 = bf16[4,256,2048]{2,1,0:T(8,128)(2,1)S(1)} fusion(f32[4,256]{1,0:T(4,128)S(1)} %get-tuple-element.732, s32[4,256]{1,0:T(4,128)S(1)} %get-tuple-element.734, f32[4,256]{1,0:T(4,128)S(1)} %get-tuple-element.736, s32[4,256]{1,0:T(4,128)S(1)} %get-tuple-element.737, f32[4,256]{1,0:T(4,128)S(1)} %get-tuple-element.739, ...), kind=kLoop, calls=%fused_computation.12.clone.clone.1.clone.1 | loop fusion | flops 100663296 | bytes 4325376 | tf_op jit(solution)/shard_map/while/body/eval_jaxpr/hqn,nhd->qhd/dot_general | solution.py:156
  232.4 5.1 %add_convert_fusion.22 = bf16[4,256,512]{2,1,0:T(8,128)(2,1)S(1)} fusion(f32[4,256]{1,0:T(4,128)S(1)} %get-tuple-element.771, s32[4,256]{1,0:T(4,128)S(1)} %get-tuple-element.772, f32[4,256]{1,0:T(4,128)S(1)} %get-tuple-element.774, s32[4,256]{1,0:T(4,128)S(1)} %get-tuple-element.775, f32[4,256]{1,0:T(4,128)S(1)} %get-tuple-element.777, ...), kind=kLoop, calls=%fused_computation.30.clone.clone.1.clone.1 | loop fusion | flops 25165824 | bytes 1179648 | tf_op jit(solution)/shard_map/while/body/eval_jaxpr/hqn,nhd->qhd/dot_general | solution.py:156
  245.6 6.5 %fusion.258 = f32[4,32,256]{2,1,0:T(8,128)} fusion(bf16[128,4,32]{0,2,1:T(8,128)(2,1)S(1)} %bitcast.884, f32[4,256]{1,0:T(4,128)S(1)} %get-tuple-element.695, s32[4,256]{1,0:T(4,128)S(1)} %get-tuple-element.696, f32[4,256]{1,0:T(4,128)S(1)} %get-tuple-element.698, s32[4,256]{1,0:T(4,128)S(1)} %get-tuple-element.699, ...), kind=kOutput, calls=%fused_computation.100.clone.1 | convolution fusion | flops 14680064 | bytes 294912 | tf_op jit(solution)/shard_map/while/body/eval_jaxpr/hqn,nhd->qhd/dot_general | solution.py:156
  256.6 18.8 %add_convert_fusion.21 = bf16[4,256,2048]{2,1,0:T(8,128)(2,1)S(1)} fusion(f32[4,256]{1,0:T(4,128)S(1)} %get-tuple-element.732, s32[4,256]{1,0:T(4,128)S(1)} %get-tuple-element.734, f32[4,256]{1,0:T(4,128)S(1)} %get-tuple-element.736, s32[4,256]{1,0:T(4,128)S(1)} %get-tuple-element.737, f32[4,256]{1,0:T(4,128)S(1)} %get-tuple-element.739, ...), kind=kLoop, calls=%fused_computation.12.clone.clone.1.clone.1 | loop fusion | flops 100663296 | bytes 4325376 | tf_op jit(solution)/shard_map/while/body/eval_jaxpr/hqn,nhd->qhd/dot_general | solution.py:156
  278.0 5.1 %add_convert_fusion.22 = bf16[4,256,512]{2,1,0:T(8,128)(2,1)S(1)} fusion(f32[4,256]{1,0:T(4,128)S(1)} %get-tuple-element.771, s32[4,256]{1,0:T(4,128)S(1)} %get-tuple-element.772, f32[4,256]{1,0:T(4,128)S(1)} %get-tuple-element.774, s32[4,256]{1,0:T(4,128)S(1)} %get-tuple-element.775, f32[4,256]{1,0:T(4,128)S(1)} %get-tuple-element.777, ...), kind=kLoop, calls=%fused_computation.30.clone.clone.1.clone.1 | loop fusion | flops 25165824 | bytes 1179648 | tf_op jit(solution)/shard_map/while/body/eval_jaxpr/hqn,nhd->qhd/dot_general | solution.py:156
  291.1 6.5 %fusion.258 = f32[4,32,256]{2,1,0:T(8,128)} fusion(bf16[128,4,32]{0,2,1:T(8,128)(2,1)S(1)} %bitcast.884, f32[4,256]{1,0:T(4,128)S(1)} %get-tuple-element.695, s32[4,256]{1,0:T(4,128)S(1)} %get-tuple-element.696, f32[4,256]{1,0:T(4,128)S(1)} %get-tuple-element.698, s32[4,256]{1,0:T(4,128)S(1)} %get-tuple-element.699, ...), kind=kOutput, calls=%fused_computation.100.clone.1 | convolution fusion | flops 14680064 | bytes 294912 | tf_op jit(solution)/shard_map/while/body/eval_jaxpr/hqn,nhd->qhd/dot_general | solution.py:156
  302.1 18.8 %add_convert_fusion.21 = bf16[4,256,2048]{2,1,0:T(8,128)(2,1)S(1)} fusion(f32[4,256]{1,0:T(4,128)S(1)} %get-tuple-element.732, s32[4,256]{1,0:T(4,128)S(1)} %get-tuple-element.734, f32[4,256]{1,0:T(4,128)S(1)} %get-tuple-element.736, s32[4,256]{1,0:T(4,128)S(1)} %get-tuple-element.737, f32[4,256]{1,0:T(4,128)S(1)} %get-tuple-element.739, ...), kind=kLoop, calls=%fused_computation.12.clone.clone.1.clone.1 | loop fusion | flops 100663296 | bytes 4325376 | tf_op jit(solution)/shard_map/while/body/eval_jaxpr/hqn,nhd->qhd/dot_general | solution.py:156
  323.5 5.1 %add_convert_fusion.22 = bf16[4,256,512]{2,1,0:T(8,128)(2,1)S(1)} fusion(f32[4,256]{1,0:T(4,128)S(1)} %get-tuple-element.771, s32[4,256]{1,0:T(4,128)S(1)} %get-tuple-element.772, f32[4,256]{1,0:T(4,128)S(1)} %get-tuple-element.774, s32[4,256]{1,0:T(4,128)S(1)} %get-tuple-element.775, f32[4,256]{1,0:T(4,128)S(1)} %get-tuple-element.777, ...), kind=kLoop, calls=%fused_computation.30.clone.clone.1.clone.1 | loop fusion | flops 25165824 | bytes 1179648 | tf_op jit(solution)/shard_map/while/body/eval_jaxpr/hqn,nhd->qhd/dot_general | solution.py:156
  (331 shorter events, 120.9 us)
Async XLA Ops:
  0.0 80.6 %copy-start = (bf16[64,16,128]{2,1,0:T(8,128)(2,1)S(1)}, bf16[64,16,128]{2,1,0:T(8,128)(2,1)}, u32[]{:S(2)}) copy-start(bf16[64,16,128]{2,1,0:T(8,128)(2,1)} %param.16) | copy-start | bytes 786436
  1.2 10.1 %copy-start.11 = (s32[32]{0:T(128)}, s32[32]{0:T(128)S(1)}, u32[]{:S(2)}) copy-start(s32[32]{0:T(128)S(1)} %convert_reduce_fusion.2) | copy-start | bytes 388
  3.0 15.6 %all-to-all-start.2 = ((s32[16,1,2]{2,1,0:T(1,128)}), s32[16,1,2]{2,1,0:T(1,128)S(1)}, u32[]{:S(2)}, u32[]{:S(2)}) async-start(s32[16,1,2]{2,1,0:T(1,128)} %bitcast.239), calls=%async_computation.2 | async-start | bytes 16384 | tf_op jit(solution)/shard_map/all_to_all | solution.py:111
  13.4 33.2 %copy-start.13 = (s32[32]{0:T(128)}, s32[32]{0:T(128)S(1)}, u32[]{:S(2)}) copy-start(s32[32]{0:T(128)S(1)} %convert_reduce_fusion.1) | copy-start | bytes 388
  14.1 32.5 %copy-start.15 = (s32[32]{0:T(128)}, s32[32]{0:T(128)S(1)}, u32[]{:S(2)}) copy-start(s32[32]{0:T(128)S(1)} %convert_reduce_fusion) | copy-start | bytes 388
  14.2 4.3 %copy-start.6 = (s32[32]{0:T(128)}, s32[32]{0:T(128)S(1)}, u32[]{:S(2)}) copy-start(s32[32]{0:T(128)S(1)} %fusion.198) | copy-start | bytes 388
  18.5 12.9 %all-to-all-start.4 = ((s32[16,1,2]{2,1,0:T(1,128)}), s32[16,1,2]{2,1,0:T(1,128)S(1)}, u32[]{:S(2)}, u32[]{:S(2)}) async-start(s32[16,1,2]{2,1,0:T(1,128)} %bitcast.248), calls=%async_computation.4 | async-start | bytes 16384 | tf_op jit(solution)/shard_map/all_to_all | solution.py:111
  31.4 10.7 %all-to-all-start.6 = ((s32[16,1,2]{2,1,0:T(1,128)}), s32[16,1,2]{2,1,0:T(1,128)S(1)}, u32[]{:S(2)}, u32[]{:S(2)}) async-start(s32[16,1,2]{2,1,0:T(1,128)} %bitcast.257), calls=%async_computation.6 | async-start | bytes 16384 | tf_op jit(solution)/shard_map/all_to_all | solution.py:111
  42.2 10.7 %all-to-all-start = ((s32[16,1,2]{2,1,0:T(1,128)}), s32[16,1,2]{2,1,0:T(1,128)S(1)}, u32[]{:S(2)}, u32[]{:S(2)}) async-start(s32[16,1,2]{2,1,0:T(1,128)} %bitcast.227), calls=%async_computation | async-start | bytes 16384 | tf_op jit(solution)/shard_map/all_to_all | solution.py:111
  52.9 12.5 %all-to-all-start.7 = ((bf16[16,2,2,2,128]{4,3,2,1,0:T(2,128)(2,1)}), bf16[16,2,2,2,128]{4,3,2,1,0:T(2,128)(2,1)S(1)}, u32[]{:S(2)}, u32[]{:S(2)}) async-start(bf16[16,2,2,2,128]{4,3,2,1,0:T(2,128)(2,1)} %broadcast_select_fusion.4), calls=%async_computation.7 | async-start | bytes 65536 | tf_op jit(solution)/shard_map/all_to_all | solution.py:120
  65.4 15.2 %copy-start.4 = (bf16[16,2,2,2,128]{4,3,2,1,0:T(2,128)(2,1)}, bf16[16,2,2,2,128]{4,3,2,1,0:T(2,128)(2,1)S(1)}, u32[]{:S(2)}) copy-start(bf16[16,2,2,2,128]{4,3,2,1,0:T(2,128)(2,1)S(1)} %all-to-all-done.7) | copy-start | bytes 98308
  65.4 11.1 %all-to-all-start.5 = ((bf16[16,2,4,4,128]{4,3,2,1,0:T(4,128)(2,1)}), bf16[16,2,4,4,128]{4,3,2,1,0:T(4,128)(2,1)S(1)}, u32[]{:S(2)}, u32[]{:S(2)}) async-start(bf16[16,2,4,4,128]{4,3,2,1,0:T(4,128)(2,1)} %select_select_fusion.2), calls=%async_computation.5 | async-start | bytes 262144 | tf_op jit(solution)/shard_map/all_to_all | solution.py:120
  76.5 15.6 %all-to-all-start.3 = ((bf16[16,2,8,8,128]{4,3,2,1,0:T(8,128)(2,1)}), bf16[16,2,8,8,128]{4,3,2,1,0:T(8,128)(2,1)S(1)}, u32[]{:S(2)}, u32[]{:S(2)}) async-start(bf16[16,2,8,8,128]{4,3,2,1,0:T(8,128)(2,1)} %select_select_fusion.1), calls=%async_computation.3 | async-start | bytes 1048576 | tf_op jit(solution)/shard_map/all_to_all | solution.py:120
  92.0 47.6 %all-to-all-start.1 = ((bf16[16,2,16,16,128]{4,3,2,1,0:T(8,128)(2,1)}), bf16[16,2,16,16,128]{4,3,2,1,0:T(8,128)(2,1)}, u32[]{:S(2)}, u32[]{:S(2)}) async-start(bf16[16,2,16,16,128]{4,3,2,1,0:T(8,128)(2,1)} %select_select_fusion), calls=%async_computation.1 | async-start | bytes 4194304 | tf_op jit(solution)/shard_map/all_to_all | solution.py:120
  97.0 4.5 %copy-start.3 = (bf16[64,16,256]{2,1,0:T(8,128)(2,1)S(1)}, bf16[64,16,256]{2,1,0:T(8,128)(2,1)}, u32[]{:S(2)}) copy-start(bf16[64,16,256]{2,1,0:T(8,128)(2,1)} %param.15) | copy-start | bytes 1572868
  101.5 6.2 %copy-start.5 = (bf16[16,2,2,2,128]{4,3,2,1,0:T(2,128)(2,1)S(1)}, bf16[16,2,2,2,128]{4,3,2,1,0:T(2,128)(2,1)}, u32[]{:S(2)}) copy-start(bf16[16,2,2,2,128]{4,3,2,1,0:T(2,128)(2,1)} %copy-done.4) | copy-start | bytes 98308
  185.7 6.3 %copy-start.1 = (f32[4,32,256]{2,1,0:T(8,128)S(1)}, f32[4,32,256]{2,1,0:T(8,128)}, u32[]{:S(2)}) copy-start(f32[4,32,256]{2,1,0:T(8,128)} %fusion.256) | copy-start | bytes 393220 | tf_op jit(solution)/shard_map/while
  185.7 6.3 %copy-start.2 = (f32[4,32,256]{2,1,0:T(8,128)S(1)}, f32[4,32,256]{2,1,0:T(8,128)}, u32[]{:S(2)}) copy-start(f32[4,32,256]{2,1,0:T(8,128)} %fusion.258) | copy-start | bytes 393220 | tf_op jit(solution)/shard_map/while
  231.2 6.3 %copy-start.1 = (f32[4,32,256]{2,1,0:T(8,128)S(1)}, f32[4,32,256]{2,1,0:T(8,128)}, u32[]{:S(2)}) copy-start(f32[4,32,256]{2,1,0:T(8,128)} %fusion.256) | copy-start | bytes 393220 | tf_op jit(solution)/shard_map/while
  231.3 6.3 %copy-start.2 = (f32[4,32,256]{2,1,0:T(8,128)S(1)}, f32[4,32,256]{2,1,0:T(8,128)}, u32[]{:S(2)}) copy-start(f32[4,32,256]{2,1,0:T(8,128)} %fusion.258) | copy-start | bytes 393220 | tf_op jit(solution)/shard_map/while
  276.8 6.3 %copy-start.1 = (f32[4,32,256]{2,1,0:T(8,128)S(1)}, f32[4,32,256]{2,1,0:T(8,128)}, u32[]{:S(2)}) copy-start(f32[4,32,256]{2,1,0:T(8,128)} %fusion.256) | copy-start | bytes 393220 | tf_op jit(solution)/shard_map/while
  276.8 6.3 %copy-start.2 = (f32[4,32,256]{2,1,0:T(8,128)S(1)}, f32[4,32,256]{2,1,0:T(8,128)}, u32[]{:S(2)}) copy-start(f32[4,32,256]{2,1,0:T(8,128)} %fusion.258) | copy-start | bytes 393220 | tf_op jit(solution)/shard_map/while
  322.3 6.3 %copy-start.1 = (f32[4,32,256]{2,1,0:T(8,128)S(1)}, f32[4,32,256]{2,1,0:T(8,128)}, u32[]{:S(2)}) copy-start(f32[4,32,256]{2,1,0:T(8,128)} %fusion.256) | copy-start | bytes 393220 | tf_op jit(solution)/shard_map/while
  322.3 6.3 %copy-start.2 = (f32[4,32,256]{2,1,0:T(8,128)S(1)}, f32[4,32,256]{2,1,0:T(8,128)}, u32[]{:S(2)}) copy-start(f32[4,32,256]{2,1,0:T(8,128)} %fusion.258) | copy-start | bytes 393220 | tf_op jit(solution)/shard_map/while
  (6 other events, 8.8 us)
where the time goes:
time: 338 us; the launch traced here: 335 us
  other arithmetic  136 us (40%)
  waiting for transfers between devices  66 us (20%)
  local copies, waits for them, and re-layouts  51.6 us (15%)
  matrix products  40.2 us (12%)
  starting transfers between devices  37.7 us (11%)
    dot_general x8, other arithmetic, block_output(): jnp.einsum('hqn,nhd->qhd', weights_px, tile_values.reshape(width_total, h...  95.6 us
    all_to_all x4, waiting for transfers between devices, on_device(): lax.all_to_all(as_sent(tuple(replies)), ('row', 'col'), split_axis=0, con...  48.7 us
    dot_general x16, matrix products, block_output(): jnp.einsum('hqn,nhd->qhd', weights_px, tile_values.reshape(width_total, h...  37.6 us
    all_to_all x4, starting transfers between devices, on_device(): lax.all_to_all(tuple(send_ids), ('row', 'col'), split_axis=0, concat_axis...  20.8 us
    all_to_all x4, waiting for transfers between devices, on_device(): lax.all_to_all(tuple(send_ids), ('row', 'col'), split_axis=0, concat_axis...  17.4 us
    all_to_all x4, starting transfers between devices, on_device(): lax.all_to_all(as_sent(tuple(replies)), ('row', 'col'), split_axis=0, con...  16.9 us
    dynamic_slice x40, local copies, waits for them, and re-layouts, on_device(): lax.map(block_output, (attend, packed, gathered[0], gathered[1], gathered...  16.3 us
    transpose x64, other arithmetic, pixel_weights(): corner_weight = (attend[:, :, point_num] * weight_row[:, :, point_num] *...  11.8 us
  transfers between devices with their start and end apart: 8, of which 8 were waited for; matrix products, arithmetic and copies ran while one was open for 9% of the time, Pallas kernels for 0%

commit v1 on v0

v1 whole, which is shorter than its diff:
```python
import functools

import jax
import jax.numpy as jnp
from jax import lax
from jax.experimental import pallas as pl
from jax.experimental.pallas import tpu as pltpu
from jax.sharding import PartitionSpec as P

LEVELS = 4
POINTS = 4
PACK = 16


def to_blocks(source, tile_rows, tile_cols, tile_side):
    channels = source.shape[2]
    shaped = source.reshape(tile_rows, tile_side, tile_cols, tile_side, channels)
    return shaped.transpose(0, 2, 1, 3, 4).reshape(
        tile_rows * tile_cols, tile_side * tile_side, channels
    )


def weight_kernel(sides, spans, per_block, head_count, query_ref, lw_ref, lb_ref, samples_ref,
                  out_ref, row_s, col_s, w0_s, w1_s, g0_s, g1_s, slot_s, mask_s):
    queries_here = query_ref.shape[1]
    hits = LEVELS * POINTS
    logits = lax.dot_general(
        lw_ref[...], query_ref[0], (((1,), (1,)), ((), ())), preferred_element_type=jnp.float32
    ) + lb_ref[...]
    logits = logits.reshape(head_count, hits, queries_here)
    shifted = jnp.exp(logits - jnp.max(logits, axis=1, keepdims=True))
    attend = shifted / jnp.sum(shifted, axis=1, keepdims=True)
    attend = attend.reshape(head_count * hits, queries_here)
    packed = samples_ref[0]
    pos_row = (packed >> 12) & 4095
    pos_col = packed & 4095
    frac_row = (pos_row & 255).astype(jnp.float32) * (1.0 / 256.0)
    frac_col = (pos_col & 255).astype(jnp.float32) * (1.0 / 256.0)
    slot_s[...] = packed >> 24
    row_s[...] = pos_row >> 8
    col_s[...] = pos_col >> 8
    w0_s[...] = attend * (1.0 - frac_row)
    w1_s[...] = attend * frac_row
    g0_s[...] = 1.0 - frac_col
    g1_s[...] = frac_col
    lane_row = lax.broadcasted_iota(jnp.int32, (PACK, queries_here), 0)
    slot_row = lax.broadcasted_iota(jnp.int32, (per_block, queries_here), 0)

    def hat(index, start, low, high):
        return jnp.where(index == start, low, jnp.where(index == start + 1, high, 0.0))

    def one_head(h, carry):
        level_off = 0
        for level_num in range(LEVELS):
            side = sides[level_num]
            span = spans[level_num]
            rows = [pl.ds(h * hits + level_num * POINTS + p, 1) for p in range(POINTS)]
            for p in range(POINTS):
                mask_s[p * per_block:(p + 1) * per_block, :] = jnp.where(
                    slot_row == slot_s[rows[p], :], 1.0, 0.0
                )
            cols = [
                hat(lane_row % side, col_s[rows[p], :], g0_s[rows[p], :], g1_s[rows[p], :])
                for p in range(POINTS)
            ]
            rows_per_chunk = PACK // side

            def chunk(step, carry, rows=rows, cols=cols, side=side, span=span,
                      level_off=level_off, rows_per_chunk=rows_per_chunk):
                parts = []
                for p in range(POINTS):
                    index = step * rows_per_chunk
                    if rows_per_chunk > 1:
                        index = index + lane_row // side
                        across = hat(index, row_s[rows[p], :], w0_s[rows[p], :], w1_s[rows[p], :])
                    else:
                        start = row_s[rows[p], :]
                        across = jnp.where(
                            start == index,
                            w0_s[rows[p], :],
                            jnp.where(start == index - 1, w1_s[rows[p], :], 0.0),
                        )
                    parts.append(cols[p] * across)
                for k in range(per_block):
                    total = parts[0] * mask_s[k:k + 1, :]
                    for p in range(1, POINTS):
                        total = total + parts[p] * mask_s[p * per_block + k:p * per_block + k + 1, :]
                    where = pl.multiple_of(level_off + k * span + step * PACK, PACK)
                    out_ref[0, h, pl.ds(where, PACK), :] = total.astype(jnp.bfloat16)
                return carry

            chunks = span // PACK
            if chunks == 1:
                chunk(0, 0)
            else:
                lax.fori_loop(0, chunks, chunk, 0)
            level_off += span * per_block
        return carry

    lax.fori_loop(0, head_count, one_head, 0)


def pick_kernel(spans, peer_count, capacity, ids_ref, l0, l1, l2, l3, out_ref, sem):
    tiles = (l0, l1, l2, l3)

    def one(slot, carry):
        peer = slot // capacity
        place = slot % capacity
        off = 0
        for level_num in range(LEVELS):
            span = spans[level_num]
            index = jnp.maximum(ids_ref[peer, level_num * capacity + place], 0)
            pltpu.make_async_copy(
                tiles[level_num].at[pl.ds(pl.multiple_of(index * span, PACK), span), :],
                out_ref.at[slot, pl.ds(off, span), :],
                sem,
            ).start()
            off += span
        return carry

    lax.fori_loop(0, peer_count * capacity, one, 0)
    pltpu.make_async_copy(out_ref, out_ref, sem).wait()


def mix_kernel(spans, per_block, head_count, head_dim, pos_ref, fetched_ref, weight_ref, out_ref,
               values, values_t, mixed, sem):
    block = pl.program_id(0)
    h = pl.program_id(1)
    blocks = pl.num_programs(0)

    def fetch(which):
        off = 0
        src = 0
        for level_num in range(LEVELS):
            span = spans[level_num]
            for k in range(per_block):
                pltpu.make_async_copy(
                    fetched_ref.at[pos_ref[level_num, which * per_block + k], pl.ds(src, span), :],
                    values.at[which % 2, pl.ds(off, span), :],
                    sem.at[which % 2],
                ).start()
                off += span
            src += span

    @pl.when((h == 0) & (block == 0))
    def _():
        fetch(block)

    @pl.when(h == 0)
    def _():
        side = block % 2
        pltpu.make_async_copy(values.at[side], values.at[side], sem.at[side]).wait()
        values_t[...] = values[side].T.reshape(values_t.shape)

        @pl.when(block + 1 < blocks)
        def _():
            fetch(block + 1)

    mixed[h] = jnp.dot(values_t[h], weight_ref[0, 0], preferred_element_type=jnp.float32)

    @pl.when(h == head_count - 1)
    def _():
        whole = mixed[...].reshape(head_count * head_dim, mixed.shape[2])
        out_ref[...] = whole.T.astype(jnp.bfloat16)


def on_device(
    queries,
    level_zero,
    level_one,
    level_two,
    level_three,
    tile_lists,
    samples,
    logit_weight,
    logit_bias,
    output_weight,
    output_bias,
    norm_gain,
    norm_shift,
):
    level_blocks = (level_zero, level_one, level_two, level_three)
    row_count = lax.axis_size("row")
    col_count = lax.axis_size("col")
    peer_count = row_count * col_count
    tile_rows, tile_cols, level_count, per_block = tile_lists.shape
    local_tiles = tile_rows * tile_cols
    requests = local_tiles * per_block
    capacity = max(2, (requests + peer_count - 1) // peer_count)
    slots = peer_count * capacity
    grid_cols = tile_cols * col_count
    channels = level_zero.shape[2]
    width_all = queries.shape[2]
    head_count = samples.shape[2] // (LEVELS * POINTS)
    head_dim = channels // head_count
    tile_side = level_zero.shape[0] // tile_rows
    pixels = tile_side * tile_side
    sides = [level_blocks[level_num].shape[0] // tile_rows for level_num in range(level_count)]
    spans = [max(PACK, side * side) for side in sides]
    tile_span = sum(spans)
    depth = per_block * tile_span

    wanted = tile_lists.transpose(2, 0, 1, 3).reshape(level_count, requests)
    grid_row = wanted // grid_cols
    grid_col = wanted % grid_cols
    owner_dev = grid_row // tile_rows * col_count + grid_col // tile_cols
    local_index = grid_row % tile_rows * tile_cols + grid_col % tile_cols
    order = jnp.arange(requests, dtype=jnp.int32)
    earlier = (owner_dev[:, :, None] == owner_dev[:, None, :]) & (order[None, :] < order[:, None])
    positions = owner_dev * capacity + jnp.sum(earlier.astype(jnp.int32), axis=2)
    slot_order = jnp.arange(slots, dtype=jnp.int32)
    named = positions[:, None, :] == slot_order[None, :, None]
    slot_table = jnp.max(jnp.where(named, local_index[:, None, :], -1), axis=2)
    send_ids = slot_table.reshape(level_count, peer_count, capacity).transpose(1, 0, 2)
    asked = lax.all_to_all(
        send_ids.reshape(peer_count, level_count * capacity),
        ("row", "col"), split_axis=0, concat_axis=0, tiled=True,
    )

    tiles_local = []
    for level_num in range(level_count):
        tiles = to_blocks(level_blocks[level_num], tile_rows, tile_cols, sides[level_num])
        short = spans[level_num] - tiles.shape[1]
        if short > 0:
            tiles = jnp.pad(tiles, ((0, 0), (0, short), (0, 0)))
        tiles_local.append(tiles.reshape(local_tiles * spans[level_num], channels))
    vmem = pl.BlockSpec(memory_space=pltpu.VMEM)
    replies = pl.pallas_call(
        functools.partial(pick_kernel, spans, peer_count, capacity),
        out_shape=jax.ShapeDtypeStruct((slots, tile_span, channels), jnp.bfloat16),
        in_specs=[pl.BlockSpec(memory_space=pltpu.SMEM)] + [vmem] * 4,
        out_specs=pl.BlockSpec(memory_space=pl.ANY),
        scratch_shapes=[pltpu.SemaphoreType.DMA],
        name="pick",
    )(asked, *tiles_local)
    fetched = lax.all_to_all(
        replies.reshape(peer_count, capacity * tile_span, channels),
        ("row", "col"), split_axis=0, concat_axis=0, tiled=True,
    ).reshape(slots, tile_span, channels)

    queries_blocked = to_blocks(queries, tile_rows, tile_cols, tile_side)
    samples_t = to_blocks(samples, tile_rows, tile_cols, tile_side).transpose(0, 2, 1)
    lanes = head_count * LEVELS * POINTS
    lane_f32 = pltpu.VMEM((lanes, pixels), jnp.float32)
    lane_i32 = pltpu.VMEM((lanes, pixels), jnp.int32)
    weights = pl.pallas_call(
        functools.partial(weight_kernel, sides, spans, per_block, head_count),
        grid=(local_tiles,),
        out_shape=jax.ShapeDtypeStruct((local_tiles, head_count, depth, pixels), jnp.bfloat16),
        in_specs=[
            pl.BlockSpec((1, pixels, width_all), lambda b: (b, 0, 0)),
            pl.BlockSpec((lanes, width_all), lambda b: (0, 0)),
            pl.BlockSpec((lanes, 1), lambda b: (0, 0)),
            pl.BlockSpec((1, lanes, pixels), lambda b: (b, 0, 0)),
        ],
        out_specs=pl.BlockSpec((1, head_count, depth, pixels), lambda b: (b, 0, 0, 0)),
        scratch_shapes=[lane_i32, lane_i32, lane_f32, lane_f32, lane_f32, lane_f32, lane_i32,
                        pltpu.VMEM((POINTS * per_block, pixels), jnp.float32)],
        compiler_params=pltpu.CompilerParams(vmem_limit_bytes=40 * 1024 * 1024),
        cost_estimate=pl.CostEstimate(
            flops=8 * local_tiles * head_count * depth * pixels * POINTS,
            bytes_accessed=2 * local_tiles * head_count * depth * pixels, transcendentals=0,
        ),
        name="weights",
    )(queries_blocked, logit_weight.T, logit_bias[:, None], samples_t)

    attn_out = pl.pallas_call(
        functools.partial(mix_kernel, spans, per_block, head_count, head_dim),
        grid_spec=pltpu.PrefetchScalarGridSpec(
            num_scalar_prefetch=1,
            grid=(local_tiles, head_count),
            in_specs=[
                pl.BlockSpec(memory_space=pl.ANY),
                pl.BlockSpec((1, 1, depth, pixels), lambda b, h, pos: (b, h, 0, 0)),
            ],
            out_specs=pl.BlockSpec((pixels, channels), lambda b, h, pos: (b, 0)),
            scratch_shapes=[
                pltpu.VMEM((2, depth, channels), jnp.bfloat16),
                pltpu.VMEM((head_count, head_dim, depth), jnp.bfloat16),
                pltpu.VMEM((head_count, head_dim, pixels), jnp.float32),
                pltpu.SemaphoreType.DMA((2,)),
            ],
        ),
        out_shape=jax.ShapeDtypeStruct((local_tiles * pixels, channels), jnp.bfloat16),
        compiler_params=pltpu.CompilerParams(
            dimension_semantics=("arbitrary", "arbitrary"), vmem_limit_bytes=24 * 1024 * 1024
        ),
        cost_estimate=pl.CostEstimate(
            flops=2 * local_tiles * depth * pixels * channels,
            bytes_accessed=2 * local_tiles * head_count * depth * pixels, transcendentals=0,
        ),
        name="mix",
    )(positions, fetched, weights)

    head_index = lax.axis_index("head")
    full_attn = lax.all_gather(attn_out, "head", axis=1, tiled=True)
    pre_norm = (
        queries_blocked.reshape(local_tiles * pixels, width_all).astype(jnp.float32)
        + jnp.dot(full_attn, output_weight, preferred_element_type=jnp.float32)
        + output_bias
    )
    row_mean = jnp.mean(pre_norm, axis=1, keepdims=True)
    centered = pre_norm - row_mean
    variance = jnp.mean(centered * centered, axis=1, keepdims=True)
    own_part = lax.dynamic_slice_in_dim(centered, head_index * channels, channels, 1)
    normalized = own_part * lax.rsqrt(variance + 1e-05)
    updated = (normalized * norm_gain + norm_shift).astype(jnp.bfloat16)
    updated = updated.reshape(tile_rows, tile_cols, tile_side, tile_side, channels).transpose(
        0, 2, 1, 3, 4
    )
    return updated.reshape(tile_rows * tile_side, tile_cols * tile_side, channels)


def solution(mesh):
    in_specs = (
        P("row", "col", None),
        P("row", "col", "head"),
        P("row", "col", "head"),
        P("row", "col", "head"),
        P("row", "col", "head"),
        P("row", "col", None, None),
        P("row", "col", "head"),
        P(None, "head"),
        P("head"),
        P(),
        P(),
        P("head"),
        P("head"),
    )
    out_specs = P("row", "col", "head")
    return jax.shard_map(
        on_device, mesh=mesh, in_specs=in_specs, out_specs=out_specs, check_vma=False
    )
```

time: 338 us -> 115 us (0.34)
  other arithmetic: 136 us -> 1.7 us
  matrix products: 40.2 us -> 0.4 us
  Pallas kernels: 0 us -> 36.3 us
  local copies, waits for them, and re-layouts: 51.6 us -> 16.3 us
  starting transfers between devices: 37.7 us -> 12.2 us
  waiting for transfers between devices: 66 us -> 45.4 us
    dot_general x8 -> x0, other arithmetic: 95.6 us -> none  [block_output(): jnp.einsum('hqn,nhd->qhd', weights_px, tile_values.reshape(width_total, h...]
    dot_general x17 -> x0, matrix products: 38.6 us -> none  [the longest x16 37.6 us: block_output(): jnp.einsum('hqn,nhd->qhd', weights_px, tile_values.reshape(width_total, h...]
    pallas_call x0 -> x3, Pallas kernels: none -> 36.3 us  [the longest x1 21 us: on_device(): pl.pallas_call(functools.partial(weight_kernel, sides, spans, per_block,...]
    all_to_all x8 -> x2, starting transfers between devices: 37.7 us -> 12.2 us  [the longest x1 8.34 us: on_device(): lax.all_to_all(send_ids.reshape(peer_count, level_count * capacity), ('ro...]
    all_to_all x8 -> x2, waiting for transfers between devices: 66 us -> 45.4 us  [the longest x1 39.5 us: on_device(): lax.all_to_all(replies.reshape(peer_count, capacity * tile_span, channels...]
    dynamic_slice x40 -> x0, local copies, waits for them, and re-layouts: 16.3 us -> none  [on_device(): lax.map(block_output, (attend, packed, gathered[0], gathered[1], gathered...]
    transpose x80 -> x0, other arithmetic: 14.7 us -> none  [the longest x64 11.8 us: pixel_weights(): corner_weight = (attend[:, :, point_num] * weight_row[:, :, point_num] *...]
    select_n x12 -> x0, other arithmetic: 11.3 us -> none  [the longest x8 7.1 us: on_device(): chosen = jnp.take(flat_tiles, positions[level_num], axis=0)]
  transfers between devices with their start and end apart: 8 -> 2, of which waited for: 8 -> 2; matrix products, arithmetic and copies ran while one was open for 9% -> 3% of each run, Pallas kernels for 0% -> 18%
where the time goes in v1:
time: 115 us
  waiting for transfers between devices  45.4 us (39%)
  Pallas kernels  36.3 us (32%)
  local copies, waits for them, and re-layouts  16.3 us (14%)
  starting transfers between devices  12.2 us (11%)
  blocking collectives  2.21 us (2%)
  other arithmetic  1.7 us (1%)
    all_to_all x1, waiting for transfers between devices, on_device(): lax.all_to_all(replies.reshape(peer_count, capacity * tile_span, channels...  39.5 us
    pallas_call x1, Pallas kernels, on_device(): pl.pallas_call(functools.partial(weight_kernel, sides, spans, per_block,...  21 us
    pallas_call x1, Pallas kernels, on_device(): pl.pallas_call(functools.partial(mix_kernel, spans, per_block, head_count...  12.6 us
    unnamed x22, local copies, waits for them, and re-layouts  10.7 us
    all_to_all x1, starting transfers between devices, on_device(): lax.all_to_all(send_ids.reshape(peer_count, level_count * capacity), ('ro...  8.34 us
    all_to_all x1, waiting for transfers between devices, on_device(): lax.all_to_all(send_ids.reshape(peer_count, level_count * capacity), ('ro...  5.98 us
    all_to_all x1, starting transfers between devices, on_device(): lax.all_to_all(replies.reshape(peer_count, capacity * tile_span, channels...  3.88 us
    pallas_call x1, Pallas kernels, on_device(): pl.pallas_call(functools.partial(pick_kernel, spans, peer_count, capacity...  2.69 us
  transfers between devices with their start and end apart: 2, of which 2 were waited for; matrix products, arithmetic and copies ran while one was open for 3% of the time, Pallas kernels for 18%

profile of v1, /device:TPU:0, one launch (start us, length us, event | category | flops | bytes accessed | tf_op | source)
XLA Modules:
  0.0 114.7 jit_solution(12602258181916821868)
XLA Ops:
  0.0 0.7 copy.30
  0.9 0.2 convert_reduce_fusion
  1.1 0.2 select_reduce_fusion
  1.3 0.1 copy.32
  1.4 0.7 copy.33
  2.1 8.3 %all-to-all-start = ((s32[16,1,8]{2,1,0:T(1,128)}), s32[16,1,8]{2,1,0:T(1,128)S(1)}, u32[]{:S(2)}, u32[]{:S(2)}) async-start(s32[16,1,8]{2,1,0:T(1,128)} %copy.33), calls=%async_computation | async-start | bytes 16384 | tf_op jit(solution)/shard_map/all_to_all | solution.py:215
  10.5 1.3 %pad.4 = bf16[4,16,128]{2,1,0:T(8,128)(2,1)} pad(bf16[4,4,128]{2,1,0:T(4,128)(2,1)} %bitcast.40, bf16[]{:T(256)} %constant.83.clone.1), padding=0_0x0_12x0_0 | pad | bytes 20482 | tf_op jit(solution)/shard_map/jit(_pad)/pad | solution.py:225
  11.8 6.0 %all-to-all-done = s32[16,1,8]{2,1,0:T(1,128)S(1)} async-done(((s32[16,1,8]{2,1,0:T(1,128)}), s32[16,1,8]{2,1,0:T(1,128)S(1)}, u32[]{:S(2)}, u32[]{:S(2)}) %all-to-all-start) | async-done | bytes 544 | tf_op jit(solution)/shard_map/all_to_all | solution.py:215
  17.7 0.6 copy-done.6
  18.3 2.7 %pick.1 = bf16[32,352,128]{2,1,0:T(8,128)(2,1)} custom-call(s32[16,8]{1,0:T(8,128)} %bitcast.36, bf16[1024,128]{1,0:T(8,128)(2,1)} %bitcast.32, bf16[256,128]{1,0:T(8,128)(2,1)} %bitcast.34, bf16[64,128]{1,0:T(8,128)(2,1)} %bitcast.37, bf16[64,128]{1,0:T(8,128)(2,1)} %bitcast.33), custom_call_target="tpu_custom_call" | custom-call | tf_op jit(solution)/shard_map/pick/pallas_call | solution.py:228
  21.1 3.9 %all-to-all-start.1 = ((bf16[16,704,128]{2,1,0:T(8,128)(2,1)}), bf16[16,704,128]{2,1,0:T(8,128)(2,1)S(1)}, u32[]{:S(2)}, u32[]{:S(2)}) async-start(bf16[16,704,128]{2,1,0:T(8,128)(2,1)} %bitcast.30), calls=%async_computation.1 | async-start | bytes 5767168 | tf_op jit(solution)/shard_map/all_to_all | solution.py:236
  25.0 1.9 %copy.36 = s32[4,256,64]{1,2,0:T(8,128)} copy(s32[4,256,64]{2,1,0:T(8,128)} %bitcast.31) | data formatting | bytes 524288 | tf_op jit(solution)/shard_map/reshape;transpose;reshape | solution.py:18
  26.9 0.7 copy.37.lb_ref
  27.6 0.9 copy-done.3
  28.6 0.8 copy-done.4
  29.3 0.8 copy-done.5
  30.1 21.0 %weights.1.weight_ref = bf16[4,4,2816,256]{3,2,1,0:T(8,128)(2,1)} custom-call(bf16[4,256,256]{2,1,0:T(8,128)(2,1)S(1)} %bitcast.26, bf16[64,256]{1,0:T(8,128)(2,1)S(1)} %bitcast.29, f32[64,1]{1,0:T(8,128)S(1)} %copy-done.4, s32[4,64,256]{2,1,0:T(8,128)S(1)} %bitcast.28), custom_call_target="tpu_custom_call" | custom-call | flops 369098752 | bytes 23068672 | tf_op jit(solution)/shard_map/weights/pallas_call | solution.py:246
  51.1 39.5 %all-to-all-done.1 = bf16[16,704,128]{2,1,0:T(8,128)(2,1)S(1)} async-done(((bf16[16,704,128]{2,1,0:T(8,128)(2,1)}), bf16[16,704,128]{2,1,0:T(8,128)(2,1)S(1)}, u32[]{:S(2)}, u32[]{:S(2)}) %all-to-all-start.1) | async-done | bytes 2883616 | tf_op jit(solution)/shard_map/all_to_all | solution.py:236
  90.6 7.6 %copy-done.1 = bf16[4,4,2816,256]{3,2,1,0:T(8,128)(2,1)S(1)} copy-done((bf16[4,4,2816,256]{3,2,1,0:T(8,128)(2,1)S(1)}, bf16[4,4,2816,256]{3,2,1,0:T(8,128)(2,1)}, u32[]{:S(2)}) %copy-start.1) | copy-done | bytes 23068696
  98.1 12.6 %mix.1 = bf16[1024,128]{1,0:T(8,128)(2,1)S(1)} custom-call(s32[4,32]{1,0:T(4,128)S(1)} %multiply_add_fusion.pos_ref, bf16[32,352,128]{2,1,0:T(8,128)(2,1)S(1)} %bitcast.25, bf16[4,4,2816,256]{3,2,1,0:T(8,128)(2,1)S(1)} %copy-done.1), custom_call_target="tpu_custom_call" | custom-call | flops 738197504 | bytes 23068672 | tf_op jit(solution)/shard_map/mix/pallas_call | solution.py:267
  110.7 2.2 %all_gather.3 = bf16[1024,256]{1,0:T(8,128)(2,1)S(1)} all-gather(bf16[1024,128]{1,0:T(8,128)(2,1)S(1)} %mix.1), channel_id=1, replica_groups=mesh['row'=4,'col'=4,'head'=2] {'head'}, dimensions={1}, use_global_device_ids=true | all-gather | bytes 786432 | tf_op jit(solution)/shard_map/all_gather | solution.py:296
  112.9 0.4 fusion.5
  113.4 0.4 multiply_reduce_fusion
  113.8 0.9 add_convert_fusion
  (24 shorter events, 0.3 us)
Async XLA Ops:
  0.0 112.9 %copy-start = (bf16[256,256]{1,0:T(8,128)(2,1)S(1)}, bf16[256,256]{1,0:T(8,128)(2,1)}, u32[]{:S(2)}) copy-start(bf16[256,256]{1,0:T(8,128)(2,1)} %param.22) | copy-start | bytes 393220
  2.1 15.6 %all-to-all-start = ((s32[16,1,8]{2,1,0:T(1,128)}), s32[16,1,8]{2,1,0:T(1,128)S(1)}, u32[]{:S(2)}, u32[]{:S(2)}) async-start(s32[16,1,8]{2,1,0:T(1,128)} %copy.33), calls=%async_computation | async-start | bytes 16384 | tf_op jit(solution)/shard_map/all_to_all | solution.py:215
  17.7 0.6 copy-start.6
  21.0 5.8 %copy-start.8 = (f32[64]{0:T(128)S(1)}, f32[64]{0:T(128)}, u32[]{:S(2)}) copy-start(f32[64]{0:T(128)} %param.21) | copy-start | bytes 772
  21.1 6.5 %copy-start.2 = (bf16[64,16,256]{2,1,0:T(8,128)(2,1)S(1)}, bf16[64,16,256]{2,1,0:T(8,128)(2,1)}, u32[]{:S(2)}) copy-start(bf16[64,16,256]{2,1,0:T(8,128)(2,1)} %param.13) | copy-start | bytes 1572868
  21.1 69.5 %all-to-all-start.1 = ((bf16[16,704,128]{2,1,0:T(8,128)(2,1)}), bf16[16,704,128]{2,1,0:T(8,128)(2,1)S(1)}, u32[]{:S(2)}, u32[]{:S(2)}) async-start(bf16[16,704,128]{2,1,0:T(8,128)(2,1)} %bitcast.30), calls=%async_computation.1 | async-start | bytes 5767168 | tf_op jit(solution)/shard_map/all_to_all | solution.py:236
  27.6 1.0 copy-start.3
  28.6 0.8 copy-start.4
  29.3 0.8 copy-start.5
  90.6 7.6 %copy-start.1 = (bf16[4,4,2816,256]{3,2,1,0:T(8,128)(2,1)S(1)}, bf16[4,4,2816,256]{3,2,1,0:T(8,128)(2,1)}, u32[]{:S(2)}) copy-start(bf16[4,4,2816,256]{3,2,1,0:T(8,128)(2,1)} %weights.1.weight_ref) | copy-start | bytes 69206016
  98.1 14.8 %copy-start.7 = (f32[256]{0:T(256)S(1)}, f32[256]{0:T(256)}, u32[]{:S(2)}) copy-start(f32[256]{0:T(256)} %param.23) | copy-start | bytes 3076
  110.7 3.0 %copy-start.9 = (f32[128]{0:T(128)S(1)}, f32[128]{0:T(128)}, u32[]{:S(2)}) copy-start(f32[128]{0:T(128)} %param.25) | copy-start | bytes 1540
  110.7 3.0 %copy-start.10 = (f32[128]{0:T(128)S(1)}, f32[128]{0:T(128)}, u32[]{:S(2)}) copy-start(f32[128]{0:T(128)} %param.24) | copy-start | bytes 1540

commit v2 on v1

v2 whole, which is shorter than its diff:
```python
import functools

import jax
import jax.numpy as jnp
from jax import lax
from jax.experimental import pallas as pl
from jax.experimental.pallas import tpu as pltpu
from jax.sharding import PartitionSpec as P

LEVELS = 4
POINTS = 4
PACK = 16
MESH = pl.DeviceIdType.MESH


def to_blocks(source, tile_rows, tile_cols, tile_side):
    channels = source.shape[2]
    shaped = source.reshape(tile_rows, tile_side, tile_cols, tile_side, channels)
    return shaped.transpose(0, 2, 1, 3, 4).reshape(
        tile_rows * tile_cols, tile_side * tile_side, channels
    )


def hat(index, start, low, high):
    return jnp.where(index == start, low, jnp.where(index == start + 1, high, 0.0))


def prepare(head_count, b, query_ref, lw_ref, lb_ref, samples_ref, point_s, corner_s):
    queries_here = query_ref.shape[1]
    hits = LEVELS * POINTS
    logits = lax.dot_general(
        lw_ref[...], query_ref[b], (((1,), (1,)), ((), ())), preferred_element_type=jnp.float32
    ) + lb_ref[...]
    logits = logits.reshape(head_count, hits, queries_here)
    shifted = jnp.exp(logits - jnp.max(logits, axis=1, keepdims=True))
    attend = shifted / jnp.sum(shifted, axis=1, keepdims=True)
    attend = attend.reshape(head_count * hits, queries_here)
    packed = samples_ref[b]
    pos_row = (packed >> 12) & 4095
    pos_col = packed & 4095
    frac_row = (pos_row & 255).astype(jnp.float32) * (1.0 / 256.0)
    frac_col = (pos_col & 255).astype(jnp.float32) * (1.0 / 256.0)
    point_s[b, 0] = packed >> 24
    point_s[b, 1] = pos_row >> 8
    point_s[b, 2] = pos_col >> 8
    corner_s[b, 0] = attend * (1.0 - frac_row)
    corner_s[b, 1] = attend * frac_row
    corner_s[b, 2] = 1.0 - frac_col
    corner_s[b, 3] = frac_col


def weigh(sides, spans, per_block, b, h, slab, point_s, corner_s, mask_s, weight_s):
    hits = LEVELS * POINTS
    queries_here = weight_s.shape[2]
    lane_row = lax.broadcasted_iota(jnp.int32, (PACK, queries_here), 0)
    slot_row = lax.broadcasted_iota(jnp.int32, (per_block, queries_here), 0)
    level_off = 0
    for level_num in range(LEVELS):
        side = sides[level_num]
        span = spans[level_num]
        rows = [pl.ds(h * hits + level_num * POINTS + p, 1) for p in range(POINTS)]
        for p in range(POINTS):
            mask_s[p * per_block:(p + 1) * per_block, :] = jnp.where(
                slot_row == point_s[b, 0, rows[p], :], 1.0, 0.0
            )
        cols = [
            hat(lane_row % side, point_s[b, 2, rows[p], :], corner_s[b, 2, rows[p], :],
                corner_s[b, 3, rows[p], :])
            for p in range(POINTS)
        ]
        rows_per_chunk = PACK // side

        def chunk(step, carry, rows=rows, cols=cols, side=side, span=span,
                  level_off=level_off, rows_per_chunk=rows_per_chunk):
            parts = []
            for p in range(POINTS):
                index = step * rows_per_chunk
                start = point_s[b, 1, rows[p], :]
                low = corner_s[b, 0, rows[p], :]
                high = corner_s[b, 1, rows[p], :]
                if rows_per_chunk > 1:
                    across = hat(index + lane_row // side, start, low, high)
                else:
                    across = jnp.where(
                        start == index, low, jnp.where(start == index - 1, high, 0.0)
                    )
                parts.append(cols[p] * across)
            for k in range(per_block):
                total = parts[0] * mask_s[k:k + 1, :]
                for p in range(1, POINTS):
                    total = total + parts[p] * mask_s[p * per_block + k:p * per_block + k + 1, :]
                where = pl.multiple_of(level_off + k * span + step * PACK, PACK)
                weight_s[slab, pl.ds(where, PACK), :] = total.astype(jnp.bfloat16)
            return carry

        chunks = span // PACK
        if chunks == 1:
            chunk(0, 0)
        else:
            lax.fori_loop(0, chunks, chunk, 0)
        level_off += span * per_block


def exchange_kernel(sides, spans, per_block, head_count, rows, cols, capacity, local_tiles, *refs):
    (table_ref, tiles_ref, query_ref, lw_ref, lb_ref, samples_ref, fetched_ref, weights_ref) = refs[:8]
    refs = refs[8:]
    held = refs[:cols - 1]
    (ids_v, stage, point_s, corner_s, mask_s, weight_s, id_send, id_recv, col_send, col_recv,
     row_send, row_recv, own_sem, ids_sem, weight_sem) = refs[cols - 1:]
    r = lax.axis_index("row")
    c = lax.axis_index("col")
    lanes_wide = tiles_ref.shape[1]
    barrier = pltpu.get_barrier_semaphore()
    for dc in range(1, cols):
        pl.semaphore_signal(barrier, inc=1, device_id={"col": lax.rem(c + dc, cols)}, device_id_type=MESH)
    for dr in range(1, rows):
        pl.semaphore_signal(barrier, inc=1, device_id={"row": lax.rem(r + dr, rows)}, device_id_type=MESH)
    pl.semaphore_wait(barrier, cols + rows - 2)

    id_copies = []
    for dr in range(1, rows):
        to = lax.rem(r + dr, rows)
        copy = pltpu.make_async_remote_copy(
            table_ref.at[to], ids_v.at[dr], id_send.at[dr], id_recv.at[dr],
            device_id={"row": to}, device_id_type=MESH,
        )
        copy.start()
        id_copies.append(copy)
    col_copies = []
    for dc in range(1, cols):
        copy = pltpu.make_async_remote_copy(
            tiles_ref, held[dc - 1], col_send.at[dc], col_recv.at[dc],
            device_id={"col": lax.rem(c + dc, cols)}, device_id_type=MESH,
        )
        copy.start()
        col_copies.append(copy)
    own_ids = pltpu.make_async_copy(table_ref.at[r], ids_v.at[0], ids_sem)
    own_ids.start()
    own_ids.wait()
    for copy in id_copies:
        copy.wait()

    def pick(dc):
        owner_col = lax.rem(c - dc + cols, cols)
        source = tiles_ref if dc == 0 else held[dc - 1]
        out_at = (r * cols + owner_col) * capacity
        copies = []
        for turn in range(rows):
            dr = (turn + 1) % rows
            for place in range(capacity):
                off = 0
                for level_num in range(LEVELS):
                    span = spans[level_num]
                    at = (owner_col * capacity + place) * LEVELS + level_num
                    asked = jnp.broadcast_to(ids_v[dr, pl.ds(at, 1), :], (PACK, lanes_wide))
                    shape = (span // PACK, PACK, lanes_wide)
                    total = None
                    for tile in range(local_tiles):
                        mask = jnp.where(asked == tile, 1.0, 0.0).astype(jnp.bfloat16)
                        first = local_tiles * off + tile * span
                        part = source[first:first + span, :].reshape(shape) * mask[None]
                        total = part if total is None else total + part
                    stage[dr, dc, place, off:off + span, :] = total.reshape(span, lanes_wide)
                    off += span
            target = fetched_ref.at[pl.ds(out_at, capacity)]
            if dr == 0:
                copy = pltpu.make_async_copy(stage.at[dr, dc], target, own_sem.at[dc])
            else:
                copy = pltpu.make_async_remote_copy(
                    stage.at[dr, dc], target, row_send.at[dr, dc], row_recv.at[dr, dc],
                    device_id={"row": lax.rem(r - dr + rows, rows)}, device_id_type=MESH,
                )
            copy.start()
            copies.append(copy)
        return copies

    copies = pick(0)

    def prepare_one(b, carry):
        prepare(head_count, b, query_ref, lw_ref, lb_ref, samples_ref, point_s, corner_s)
        return carry

    lax.fori_loop(0, local_tiles, prepare_one, 0)

    def store(step, slab):
        return pltpu.make_async_copy(
            weight_s.at[slab], weights_ref.at[step // head_count, step % head_count],
            weight_sem.at[slab],
        )

    def weigh_one(step, carry):
        slab = step % 2

        @pl.when(step >= 2)
        def _():
            store(step - 2, slab).wait()

        weigh(sides, spans, per_block, step // head_count, step % head_count, slab,
              point_s, corner_s, mask_s, weight_s)
        store(step, slab).start()
        return carry

    steps = local_tiles * head_count
    done = 0
    for dc in range(1, cols):
        until = steps * dc // (cols - 1)
        if until > done:
            lax.fori_loop(done, until, weigh_one, 0)
        done = until
        col_copies[dc - 1].wait()
        copies += pick(dc)
    for step in range(max(0, steps - 2), steps):
        store(step, step % 2).wait()
    for copy in copies:
        copy.wait()


def mix_kernel(spans, per_block, head_count, head_dim, pos_ref, fetched_ref, weight_ref, out_ref,
               values, values_t, mixed, sem):
    block = pl.program_id(0)
    h = pl.program_id(1)
    blocks = pl.num_programs(0)

    def fetch(which):
        off = 0
        src = 0
        for level_num in range(LEVELS):
            span = spans[level_num]
            for k in range(per_block):
                pltpu.make_async_copy(
                    fetched_ref.at[pos_ref[level_num, which * per_block + k], pl.ds(src, span), :],
                    values.at[which % 2, pl.ds(off, span), :],
                    sem.at[which % 2],
                ).start()
                off += span
            src += span

    @pl.when((h == 0) & (block == 0))
    def _():
        fetch(block)

    @pl.when(h == 0)
    def _():
        side = block % 2
        pltpu.make_async_copy(values.at[side], values.at[side], sem.at[side]).wait()
        values_t[...] = values[side].T.reshape(values_t.shape)

        @pl.when(block + 1 < blocks)
        def _():
            fetch(block + 1)

    mixed[h] = jnp.dot(values_t[h], weight_ref[0, 0], preferred_element_type=jnp.float32)

    @pl.when(h == head_count - 1)
    def _():
        whole = mixed[...].reshape(head_count * head_dim, mixed.shape[2])
        out_ref[...] = whole.T.astype(jnp.bfloat16)


def on_device(
    queries,
    level_zero,
    level_one,
    level_two,
    level_three,
    tile_lists,
    samples,
    logit_weight,
    logit_bias,
    output_weight,
    output_bias,
    norm_gain,
    norm_shift,
):
    level_blocks = (level_zero, level_one, level_two, level_three)
    row_count = lax.axis_size("row")
    col_count = lax.axis_size("col")
    peer_count = row_count * col_count
    tile_rows, tile_cols, level_count, per_block = tile_lists.shape
    local_tiles = tile_rows * tile_cols
    requests = local_tiles * per_block
    capacity = max(2, (requests + peer_count - 1) // peer_count)
    slots = peer_count * capacity
    grid_cols = tile_cols * col_count
    channels = level_zero.shape[2]
    width_all = queries.shape[2]
    head_count = samples.shape[2] // (LEVELS * POINTS)
    head_dim = channels // head_count
    tile_side = level_zero.shape[0] // tile_rows
    pixels = tile_side * tile_side
    sides = [level_blocks[level_num].shape[0] // tile_rows for level_num in range(level_count)]
    spans = [max(PACK, side * side) for side in sides]
    tile_span = sum(spans)
    depth = per_block * tile_span

    wanted = tile_lists.transpose(2, 0, 1, 3).reshape(level_count, requests)
    grid_row = wanted // grid_cols
    grid_col = wanted % grid_cols
    owner_dev = grid_row // tile_rows * col_count + grid_col // tile_cols
    local_index = grid_row % tile_rows * tile_cols + grid_col % tile_cols
    order = jnp.arange(requests, dtype=jnp.int32)
    earlier = (owner_dev[:, :, None] == owner_dev[:, None, :]) & (order[None, :] < order[:, None])
    positions = owner_dev * capacity + jnp.sum(earlier.astype(jnp.int32), axis=2)
    slot_order = jnp.arange(slots, dtype=jnp.int32)
    named = positions[:, None, :] == slot_order[None, :, None]
    slot_table = jnp.max(jnp.where(named, local_index[:, None, :], -1), axis=2)
    table = jnp.maximum(slot_table, 0).reshape(level_count, row_count, col_count * capacity)
    table = table.transpose(1, 2, 0).reshape(row_count, col_count * capacity * level_count, 1)
    table_rows = table.shape[1]
    table = jnp.broadcast_to(table, (row_count, table_rows, channels))

    tiles_local = []
    for level_num in range(level_count):
        tiles = to_blocks(level_blocks[level_num], tile_rows, tile_cols, sides[level_num])
        short = spans[level_num] - tiles.shape[1]
        if short > 0:
            tiles = jnp.pad(tiles, ((0, 0), (0, short), (0, 0)))
        tiles_local.append(tiles.reshape(local_tiles * spans[level_num], channels))
    tiles_local = jnp.concatenate(tiles_local, axis=0)

    queries_blocked = to_blocks(queries, tile_rows, tile_cols, tile_side)
    samples_t = to_blocks(samples, tile_rows, tile_cols, tile_side).transpose(0, 2, 1)
    lanes = head_count * LEVELS * POINTS
    vmem = pl.BlockSpec(memory_space=pltpu.VMEM)
    whole = pl.BlockSpec(memory_space=pl.ANY)
    dma = pltpu.SemaphoreType.DMA
    fetched, weights = pl.pallas_call(
        functools.partial(exchange_kernel, sides, spans, per_block, head_count, row_count,
                          col_count, capacity, local_tiles),
        out_shape=(
            jax.ShapeDtypeStruct((slots, tile_span, channels), jnp.bfloat16),
            jax.ShapeDtypeStruct((local_tiles, head_count, depth, pixels), jnp.bfloat16),
        ),
        in_specs=[vmem] * 6,
        out_specs=(whole, whole),
        scratch_shapes=[
            pltpu.VMEM((local_tiles * tile_span, channels), jnp.bfloat16)
            for _ in range(col_count - 1)
        ] + [
            pltpu.VMEM((row_count, table_rows, channels), jnp.int32),
            pltpu.VMEM((row_count, col_count, capacity, tile_span, channels), jnp.bfloat16),
            pltpu.VMEM((local_tiles, 3, lanes, pixels), jnp.int32),
            pltpu.VMEM((local_tiles, 4, lanes, pixels), jnp.float32),
            pltpu.VMEM((POINTS * per_block, pixels), jnp.float32),
            pltpu.VMEM((2, depth, pixels), jnp.bfloat16),
            dma((row_count,)), dma((row_count,)), dma((col_count,)), dma((col_count,)),
            dma((row_count, col_count)), dma((row_count, col_count)), dma((col_count,)),
            dma, dma((2,)),
        ],
        compiler_params=pltpu.CompilerParams(
            collective_id=0, has_side_effects=True, vmem_limit_bytes=60 * 1024 * 1024
        ),
        cost_estimate=pl.CostEstimate(
            flops=8 * local_tiles * head_count * depth * pixels * POINTS,
            bytes_accessed=2 * local_tiles * head_count * depth * pixels, transcendentals=0,
        ),
        name="exchange",
    )(table, tiles_local, queries_blocked, logit_weight.T, logit_bias[:, None], samples_t)

    attn_out = pl.pallas_call(
        functools.partial(mix_kernel, spans, per_block, head_count, head_dim),
        grid_spec=pltpu.PrefetchScalarGridSpec(
            num_scalar_prefetch=1,
            grid=(local_tiles, head_count),
            in_specs=[
                pl.BlockSpec(memory_space=pl.ANY),
                pl.BlockSpec((1, 1, depth, pixels), lambda b, h, pos: (b, h, 0, 0)),
            ],
            out_specs=pl.BlockSpec((pixels, channels), lambda b, h, pos: (b, 0)),
            scratch_shapes=[
                pltpu.VMEM((2, depth, channels), jnp.bfloat16),
                pltpu.VMEM((head_count, head_dim, depth), jnp.bfloat16),
                pltpu.VMEM((head_count, head_dim, pixels), jnp.float32),
                pltpu.SemaphoreType.DMA((2,)),
            ],
        ),
        out_shape=jax.ShapeDtypeStruct((local_tiles * pixels, channels), jnp.bfloat16),
        compiler_params=pltpu.CompilerParams(
            dimension_semantics=("arbitrary", "arbitrary"), vmem_limit_bytes=60 * 1024 * 1024
        ),
        cost_estimate=pl.CostEstimate(
            flops=2 * local_tiles * depth * pixels * channels,
            bytes_accessed=2 * local_tiles * head_count * depth * pixels, transcendentals=0,
        ),
        name="mix",
    )(positions, fetched, weights)

    head_index = lax.axis_index("head")
    full_attn = lax.all_gather(attn_out, "head", axis=1, tiled=True)
    pre_norm = (
        queries_blocked.reshape(local_tiles * pixels, width_all).astype(jnp.float32)
        + jnp.dot(full_attn, output_weight, preferred_element_type=jnp.float32)
        + output_bias
    )
    row_mean = jnp.mean(pre_norm, axis=1, keepdims=True)
    centered = pre_norm - row_mean
    variance = jnp.mean(centered * centered, axis=1, keepdims=True)
    own_part = lax.dynamic_slice_in_dim(centered, head_index * channels, channels, 1)
    normalized = own_part * lax.rsqrt(variance + 1e-05)
    updated = (normalized * norm_gain + norm_shift).astype(jnp.bfloat16)
    updated = updated.reshape(tile_rows, tile_cols, tile_side, tile_side, channels).transpose(
        0, 2, 1, 3, 4
    )
    return updated.reshape(tile_rows * tile_side, tile_cols * tile_side, channels)


def solution(mesh):
    in_specs = (
        P("row", "col", None),
        P("row", "col", "head"),
        P("row", "col", "head"),
        P("row", "col", "head"),
        P("row", "col", "head"),
        P("row", "col", None, None),
        P("row", "col", "head"),
        P(None, "head"),
        P("head"),
        P(),
        P(),
        P("head"),
        P("head"),
    )
    out_specs = P("row", "col", "head")
    return jax.shard_map(
        on_device, mesh=mesh, in_specs=in_specs, out_specs=out_specs, check_vma=False
    )
```

time: 115 us -> 85.7 us (0.75)
  the two profiles are of different devices: /device:TPU:0 before, /device:TPU:25 now
where the time goes in v2:
time: 85.7 us; the launch traced here: 85.1 us
  Pallas kernels  71.8 us (84%)
  local copies, waits for them, and re-layouts  5.82 us (7%)
  other arithmetic  3.49 us (4%)
  blocking collectives  3.42 us (4%)
    pallas_call x1, Pallas kernels, on_device(): pl.pallas_call(functools.partial(exchange_kernel, sides, spans, per_block...  53.2 us
    pallas_call x1, Pallas kernels, on_device(): pl.pallas_call(functools.partial(mix_kernel, spans, per_block, head_count...  18.6 us
    all_gather x1, blocking collectives, on_device(): full_attn = lax.all_gather(attn_out, 'head', axis=1, tiled=True)  3.42 us
    another operation x1, local copies, waits for them, and re-layouts, to_blocks(): shaped.transpose(0, 2, 1, 3, 4)  1.93 us
    concatenate x1, other arithmetic, on_device(): tiles_local = jnp.concatenate(tiles_local, axis=0)  1.79 us

profile of v2, /device:TPU:25, one launch (start us, length us, event | category | flops | bytes accessed | tf_op | source)
XLA Modules:
  0.0 85.1 jit_solution(9041182602761279117)
XLA Ops:
  0.0 0.0 copy-start
  0.0 0.0 copy-start.5
  0.0 0.0 copy-start.4
  0.0 0.8 copy.21
  0.8 0.1 reshape.212
  0.9 0.2 convert_reduce_fusion
  1.1 0.0 copy-start.2
  1.2 0.1 select_reduce_fusion
  1.3 0.1 max.9
  1.4 0.1 copy.22
  1.5 0.1 broadcast_in_dim.20
  1.6 0.7 broadcast_in_dim.21.refs_0_
  2.3 0.7 pad.4
  3.0 1.8 %pad_maximum_fusion.refs_1_ = bf16[1408,128]{1,0:T(8,128)(2,1)} fusion(bf16[64,128]{1,0:T(8,128)(2,1)S(1)} %bitcast.24, bf16[64,128]{1,0:T(8,128)(2,1)} %bitcast.27, bf16[256,128]{1,0:T(8,128)(2,1)} %bitcast.25, bf16[1024,128]{1,0:T(8,128)(2,1)} %bitcast.23), kind=kLoop, calls=%fused_computation.5 | loop fusion | flops 1441792 | bytes 720896 | tf_op jit(solution)/shard_map/concatenate | solution.py:319
  4.8 1.9 %copy.23 = s32[4,256,64]{1,2,0:T(8,128)} copy(s32[4,256,64]{2,1,0:T(8,128)} %bitcast.19) | data formatting | bytes 524288 | tf_op jit(solution)/shard_map/reshape;transpose;reshape | solution.py:19
  6.7 1.3 %copy.24.refs_4_ = f32[64,1]{1,0:T(8,128)} copy(f32[64,1]{0,1:T(1,128)} %bitcast.30) | data formatting | bytes 512 | tf_op jit(solution)/shard_map/broadcast_in_dim | solution.py:358
  8.1 53.2 %exchange.1 = (bf16[32,352,128]{2,1,0:T(8,128)(2,1)}, bf16[4,4,2816,256]{3,2,1,0:T(8,128)(2,1)}) custom-call(s32[4,32,128]{2,1,0:T(8,128)} %broadcast_in_dim.21.refs_0_, bf16[1408,128]{1,0:T(8,128)(2,1)} %pad_maximum_fusion.refs_1_, bf16[4,256,256]{2,1,0:T(8,128)(2,1)} %bitcast.20, bf16[64,256]{1,0:T(8,128)(2,1)} %bitcast.31, f32[64,1]{1,0:T(8,128)} %copy.24.refs_4_, ...), custom_call_target="tpu_custom_call" | custom-call | flops 369098752 | bytes 23068672 | tf_op jit(solution)/shard_map/exchange/pallas_call | solution.py:327
  61.3 0.0 copy-done.2
  61.3 18.6 %mix.1 = bf16[1024,128]{1,0:T(8,128)(2,1)} custom-call(s32[4,32]{1,0:T(4,128)} %copy-done.2, bf16[32,352,128]{2,1,0:T(8,128)(2,1)} %get-tuple-element.7.fetched_ref, bf16[4,4,2816,256]{3,2,1,0:T(8,128)(2,1)} %get-tuple-element.8.weight_ref), custom_call_target="tpu_custom_call" | custom-call | flops 738197504 | bytes 23068672 | tf_op jit(solution)/shard_map/mix/pallas_call | solution.py:360
  79.9 3.4 %all_gather.3 = bf16[1024,256]{1,0:T(8,128)(2,1)S(1)} all-gather(bf16[1024,128]{1,0:T(8,128)(2,1)} %mix.1), channel_id=1, replica_groups=mesh['row'=4,'col'=4,'head'=2] {'head'}, dimensions={1}, use_global_device_ids=true | all-gather | bytes 786432 | tf_op jit(solution)/shard_map/all_gather | solution.py:389
  83.3 0.0 copy-done.3
  83.3 0.4 fusion.5
  83.7 0.4 multiply_reduce_fusion
  84.1 0.9 %add_convert_fusion = bf16[1024,128]{1,0:T(8,128)(2,1)} fusion(f32[1024,256]{1,0:T(8,128)S(1)} %get-tuple-element.10, s32[]{:T(128)S(6)} %select_n.83, f32[128]{0:T(128)S(1)} %copy-done.4, f32[128]{0:T(128)S(1)} %copy-done.5, f32[1024]{0:T(1024)S(1)} %add_rsqrt_fusion), kind=kLoop, calls=%fused_computation.3 | loop fusion | flops 524288 | bytes 791556 | tf_op jit(solution)/shard_map/convert_element_type | solution.py:400
  (12 shorter events, 0.1 us)
Async XLA Ops:
  0.0 83.3 %copy-start = (bf16[256,256]{1,0:T(8,128)(2,1)S(1)}, bf16[256,256]{1,0:T(8,128)(2,1)}, u32[]{:S(2)}) copy-start(bf16[256,256]{1,0:T(8,128)(2,1)} %param.22) | copy-start | bytes 393220
  0.0 83.3 %copy-start.1 = (bf16[64,16,256]{2,1,0:T(8,128)(2,1)S(1)}, bf16[64,16,256]{2,1,0:T(8,128)(2,1)}, u32[]{:S(2)}) copy-start(bf16[64,16,256]{2,1,0:T(8,128)(2,1)} %param.13) | copy-start | bytes 1572868
  0.0 83.3 %copy-start.3 = (f32[256]{0:T(256)S(1)}, f32[256]{0:T(256)}, u32[]{:S(2)}) copy-start(f32[256]{0:T(256)} %param.23) | copy-start | bytes 3076
  0.0 84.1 %copy-start.5 = (f32[128]{0:T(128)S(1)}, f32[128]{0:T(128)}, u32[]{:S(2)}) copy-start(f32[128]{0:T(128)} %param.24) | copy-start | bytes 1540
  0.0 84.1 %copy-start.4 = (f32[128]{0:T(128)S(1)}, f32[128]{0:T(128)}, u32[]{:S(2)}) copy-start(f32[128]{0:T(128)} %param.25) | copy-start | bytes 1540
  1.1 60.2 %copy-start.2 = (s32[4,32]{1,0:T(4,128)}, s32[4,32]{1,0:T(4,128)S(1)}, u32[]{:S(2)}) copy-start(s32[4,32]{1,0:T(4,128)S(1)} %multiply_add_fusion.pos_ref) | copy-start | bytes 1540

commit v3 on v2

--- a/solution.py
+++ b/solution.py
@@ -35,7 +35,7 @@
     shifted = jnp.exp(logits - jnp.max(logits, axis=1, keepdims=True))
     attend = shifted / jnp.sum(shifted, axis=1, keepdims=True)
     attend = attend.reshape(head_count * hits, queries_here)
-    packed = samples_ref[b]
+    packed = samples_ref[b].T
     pos_row = (packed >> 12) & 4095
     pos_col = packed & 4095
     frac_row = (pos_row & 255).astype(jnp.float32) * (1.0 / 256.0)
@@ -215,7 +215,8 @@
         copy.wait()
 
 
-def mix_kernel(spans, per_block, head_count, head_dim, pos_ref, fetched_ref, weight_ref, out_ref,
+def mix_kernel(spans, per_block, head_count, head_dim, pos_ref, fetched_ref, upper_ref, lower_ref,
+               out_ref,
                values, values_t, mixed, sem):
     block = pl.program_id(0)
     h = pl.program_id(1)
@@ -249,7 +250,10 @@
         def _():
             fetch(block + 1)
 
-    mixed[h] = jnp.dot(values_t[h], weight_ref[0, 0], preferred_element_type=jnp.float32)
+    half = upper_ref.shape[2]
+    mixed[h] = jnp.dot(
+        values_t[h, :, :half], upper_ref[0, 0], preferred_element_type=jnp.float32
+    ) + jnp.dot(values_t[h, :, half:], lower_ref[0, 0], preferred_element_type=jnp.float32)
 
     @pl.when(h == head_count - 1)
     def _():
@@ -319,7 +323,7 @@
     tiles_local = jnp.concatenate(tiles_local, axis=0)
 
     queries_blocked = to_blocks(queries, tile_rows, tile_cols, tile_side)
-    samples_t = to_blocks(samples, tile_rows, tile_cols, tile_side).transpose(0, 2, 1)
+    samples_blocked = to_blocks(samples, tile_rows, tile_cols, tile_side)
     lanes = head_count * LEVELS * POINTS
     vmem = pl.BlockSpec(memory_space=pltpu.VMEM)
     whole = pl.BlockSpec(memory_space=pl.ANY)
@@ -355,7 +359,7 @@
             bytes_accessed=2 * local_tiles * head_count * depth * pixels, transcendentals=0,
         ),
         name="exchange",
-    )(table, tiles_local, queries_blocked, logit_weight.T, logit_bias[:, None], samples_t)
+    )(table, tiles_local, queries_blocked, logit_weight.T, logit_bias[:, None], samples_blocked)
 
     attn_out = pl.pallas_call(
         functools.partial(mix_kernel, spans, per_block, head_count, head_dim),
@@ -364,7 +368,8 @@
             grid=(local_tiles, head_count),
             in_specs=[
                 pl.BlockSpec(memory_space=pl.ANY),
-                pl.BlockSpec((1, 1, depth, pixels), lambda b, h, pos: (b, h, 0, 0)),
+                pl.BlockSpec((1, 1, depth // 2, pixels), lambda b, h, pos: (b, h, 0, 0)),
+                pl.BlockSpec((1, 1, depth // 2, pixels), lambda b, h, pos: (b, h, 1, 0)),
             ],
             out_specs=pl.BlockSpec((pixels, channels), lambda b, h, pos: (b, 0)),
             scratch_shapes=[
@@ -383,7 +388,7 @@
             bytes_accessed=2 * local_tiles * head_count * depth * pixels, transcendentals=0,
         ),
         name="mix",
-    )(positions, fetched, weights)
+    )(positions, fetched, weights, weights)
 
     head_index = lax.axis_index("head")
     full_attn = lax.all_gather(attn_out, "head", axis=1, tiled=True)

time: 85.7 us -> 83.6 us (0.975)
  local copies, waits for them, and re-layouts: 5.82 us -> 3.88 us
    another operation x1 -> x0, local copies, waits for them, and re-layouts: 1.93 us -> none  [to_blocks(): shaped.transpose(0, 2, 1, 3, 4)]
where the time goes in v3:
time: 83.6 us; the launch traced here: 83 us
  Pallas kernels  71.7 us (86%)
  local copies, waits for them, and re-layouts  3.88 us (5%)
  other arithmetic  3.49 us (4%)
  blocking collectives  3.41 us (4%)
    pallas_call x1, Pallas kernels, on_device(): pl.pallas_call(functools.partial(exchange_kernel, sides, spans, per_block...  53.3 us
    pallas_call x1, Pallas kernels, on_device(): pl.pallas_call(functools.partial(mix_kernel, spans, per_block, head_count...  18.3 us
    all_gather x1, blocking collectives, on_device(): full_attn = lax.all_gather(attn_out, 'head', axis=1, tiled=True)  3.41 us
    concatenate x1, other arithmetic, on_device(): tiles_local = jnp.concatenate(tiles_local, axis=0)  1.79 us

profile of v3, /device:TPU:25, one launch (start us, length us, event | category | flops | bytes accessed | tf_op | source)
XLA Modules:
  0.0 83.0 jit_solution(18260545726815025878)
XLA Ops:
  0.0 0.7 copy.20
  0.7 0.1 reshape.212
  0.9 0.2 convert_reduce_fusion
  1.1 0.1 select_reduce_fusion
  1.3 0.1 max.9
  1.3 0.1 copy.21
  1.4 0.1 broadcast_in_dim.20
  1.5 0.7 broadcast_in_dim.21.refs_0_
  2.3 0.7 pad.4
  2.9 1.8 %pad_maximum_fusion.refs_1_ = bf16[1408,128]{1,0:T(8,128)(2,1)} fusion(bf16[64,128]{1,0:T(8,128)(2,1)S(1)} %bitcast.22, bf16[64,128]{1,0:T(8,128)(2,1)} %bitcast.26, bf16[256,128]{1,0:T(8,128)(2,1)} %bitcast.23, bf16[1024,128]{1,0:T(8,128)(2,1)} %bitcast.21), kind=kLoop, calls=%fused_computation.5 | loop fusion | flops 1441792 | bytes 720896 | tf_op jit(solution)/shard_map/concatenate | solution.py:323
  4.7 1.3 %copy.22.refs_4_ = f32[64,1]{1,0:T(8,128)} copy(f32[64,1]{0,1:T(1,128)} %bitcast.29) | data formatting | bytes 512 | tf_op jit(solution)/shard_map/broadcast_in_dim | solution.py:362
  6.1 53.3 %exchange.1 = (bf16[32,352,128]{2,1,0:T(8,128)(2,1)}, bf16[4,4,2816,256]{3,2,1,0:T(8,128)(2,1)}) custom-call(s32[4,32,128]{2,1,0:T(8,128)} %broadcast_in_dim.21.refs_0_, bf16[1408,128]{1,0:T(8,128)(2,1)} %pad_maximum_fusion.refs_1_, bf16[4,256,256]{2,1,0:T(8,128)(2,1)} %bitcast.18, bf16[64,256]{1,0:T(8,128)(2,1)} %bitcast.24, f32[64,1]{1,0:T(8,128)} %copy.22.refs_4_, ...), custom_call_target="tpu_custom_call" | custom-call | flops 369098752 | bytes 23068672 | tf_op jit(solution)/shard_map/exchange/pallas_call | solution.py:331
  59.4 0.0 copy-done.2
  59.4 0.0 copy-start.1
  59.5 0.0 copy-start.3
  59.5 0.0 copy-start.4
  59.5 0.0 copy-start.5
  59.5 18.3 %mix.1 = bf16[1024,128]{1,0:T(8,128)(2,1)} custom-call(s32[4,32]{1,0:T(4,128)} %copy-done.2, bf16[32,352,128]{2,1,0:T(8,128)(2,1)} %get-tuple-element.7.fetched_ref, bf16[4,4,2816,256]{3,2,1,0:T(8,128)(2,1)} %get-tuple-element.8.upper_ref.lower_ref, bf16[4,4,2816,256]{3,2,1,0:T(8,128)(2,1)} %get-tuple-element.8.upper_ref.lower_ref), custom_call_target="tpu_custom_call" | custom-call | flops 738197504 | bytes 23068672 | tf_op jit(solution)/shard_map/mix/pallas_call | solution.py:364
  77.8 3.4 %all_gather.3 = bf16[1024,256]{1,0:T(8,128)(2,1)S(1)} all-gather(bf16[1024,128]{1,0:T(8,128)(2,1)} %mix.1), channel_id=1, replica_groups=mesh['row'=4,'col'=4,'head'=2] {'head'}, dimensions={1}, use_global_device_ids=true | all-gather | bytes 786432 | tf_op jit(solution)/shard_map/all_gather | solution.py:394
  81.2 0.0 copy-done
  81.2 0.0 copy-done.3
  81.2 0.4 fusion.5
  81.7 0.4 multiply_reduce_fusion
  82.1 0.9 %add_convert_fusion = bf16[1024,128]{1,0:T(8,128)(2,1)} fusion(f32[1024,256]{1,0:T(8,128)S(1)} %get-tuple-element.10, s32[]{:T(128)S(6)} %select_n.83, f32[128]{0:T(128)S(1)} %copy-done.4, f32[128]{0:T(128)S(1)} %copy-done.5, f32[1024]{0:T(1024)S(1)} %add_rsqrt_fusion), kind=kLoop, calls=%fused_computation.3 | loop fusion | flops 524288 | bytes 791556 | tf_op jit(solution)/shard_map/convert_element_type | solution.py:405
  (11 shorter events, 0.1 us)
Async XLA Ops:
  0.0 81.2 %copy-start = (bf16[256,256]{1,0:T(8,128)(2,1)S(1)}, bf16[256,256]{1,0:T(8,128)(2,1)}, u32[]{:S(2)}) copy-start(bf16[256,256]{1,0:T(8,128)(2,1)} %param.22) | copy-start | bytes 393220
  1.1 58.3 %copy-start.2 = (s32[4,32]{1,0:T(4,128)}, s32[4,32]{1,0:T(4,128)S(1)}, u32[]{:S(2)}) copy-start(s32[4,32]{1,0:T(4,128)S(1)} %multiply_add_fusion.pos_ref) | copy-start | bytes 1540
  59.4 21.8 %copy-start.1 = (bf16[64,16,256]{2,1,0:T(8,128)(2,1)S(1)}, bf16[64,16,256]{2,1,0:T(8,128)(2,1)}, u32[]{:S(2)}) copy-start(bf16[64,16,256]{2,1,0:T(8,128)(2,1)} %param.13) | copy-start | bytes 1572868
  59.5 21.8 %copy-start.3 = (f32[256]{0:T(256)S(1)}, f32[256]{0:T(256)}, u32[]{:S(2)}) copy-start(f32[256]{0:T(256)} %param.23) | copy-start | bytes 3076
  59.5 22.6 %copy-start.4 = (f32[128]{0:T(128)S(1)}, f32[128]{0:T(128)}, u32[]{:S(2)}) copy-start(f32[128]{0:T(128)} %param.25) | copy-start | bytes 1540
  59.5 22.6 %copy-start.5 = (f32[128]{0:T(128)S(1)}, f32[128]{0:T(128)}, u32[]{:S(2)}) copy-start(f32[128]{0:T(128)} %param.24) | copy-start | bytes 1540
